TPU v7x, 128 devices: a whole 4x4x4 slice. The times are simulated.
128 devices in a mesh: dp: 1, ep: 128 (over z, y, x, core).
Axes of the slice: x: 4, y: 4, z: 4, core: 2. Of those that a mesh axis runs over, the one named last changes fastest.
Arguments:
- tokens: bfloat16 [8192, 2048], P(('dp', 'ep'))
- expert_ids: int32 [8192, 8], P(('dp', 'ep'))
- gate_w: float32 [8192, 8], P(('dp', 'ep'))
- route_counts: int32 [128, 128], P(('dp', 'ep'))
- w_gate: bfloat16 [128, 2048, 768], P('ep')
- w_up: bfloat16 [128, 2048, 768], P('ep')
- w_down: bfloat16 [128, 768, 2048], P('ep')
Outputs:
- output: bfloat16 [8192, 2048], P(('dp', 'ep'))
All inputs are finite; a program needn't handle non-finite values.
Results may differ from a plain program's by a relative error of at most 0.00369945.
Values are sent between devices in bfloat16 or wider.
A program may use at most 1 GiB of HBM per device.

v0:
```python
import jax
import jax.numpy as jnp
from jax import lax
from jax.sharding import PartitionSpec as P


def place_rows(expert_ids, counts_row, cap_rows, n_exp):
    tok_n, top_n = expert_ids.shape
    flat_ids = expert_ids.reshape(tok_n * top_n)
    onehot = (flat_ids[:, None] == jnp.arange(n_exp)[None, :]).astype(jnp.int32)
    before = jnp.cumsum(onehot, axis=0) - onehot
    slot_idx = jnp.sum(before * onehot, axis=1)
    row_limit = jnp.sum(onehot * counts_row[None, :], axis=1)
    buf_pos = jnp.where(slot_idx < row_limit, flat_ids * cap_rows + slot_idx, -1)
    return buf_pos.reshape(tok_n, top_n)


def expert_ffn(rows_in, w_gate, w_up, w_down):
    act_a = jnp.einsum("erd,edf->erf", rows_in, w_gate, preferred_element_type=jnp.float32)
    act_b = jnp.einsum("erd,edf->erf", rows_in, w_up, preferred_element_type=jnp.float32)
    hidden = (jax.nn.silu(act_a) * act_b).astype(jnp.bfloat16)
    return jnp.einsum("erf,efd->erd", hidden, w_down, preferred_element_type=jnp.float32).astype(jnp.bfloat16)


def solution(mesh):
    group_size = mesh.shape["ep"]
    row_spec = P(("dp", "ep"))

    def local_step(tokens, expert_ids, gate_w, route_counts, w_gate, w_up, w_down):
        tok_n = expert_ids.shape[0]
        n_local = w_gate.shape[0]
        model_dim = w_gate.shape[1]
        n_exp = n_local * group_size
        cap_rows = tok_n // 2
        buf_pos = place_rows(expert_ids, route_counts[0], cap_rows, n_exp)
        disp_mat = jnp.any(jnp.arange(n_exp * cap_rows)[:, None, None] == buf_pos[None, :, :], axis=2).astype(jnp.bfloat16)
        packed = jnp.dot(disp_mat, tokens, preferred_element_type=jnp.float32).astype(jnp.bfloat16)
        packed = packed.reshape(group_size, n_local, cap_rows, model_dim)
        arrived = lax.all_to_all(packed, "ep", 0, 2, tiled=True)
        expert_out = expert_ffn(arrived.reshape(n_local, group_size * cap_rows, model_dim), w_gate, w_up, w_down)
        returned = lax.all_to_all(expert_out.reshape(1, n_local, group_size * cap_rows, model_dim), "ep", 2, 0, tiled=True)
        picked = jnp.take(returned.reshape(n_exp * cap_rows, model_dim), jnp.maximum(buf_pos, 0), axis=0)
        weights = jnp.where(buf_pos >= 0, gate_w, 0.0)
        total_f32 = tokens.astype(jnp.float32) + jnp.sum(weights[:, :, None] * picked.astype(jnp.float32), axis=1)
        return total_f32.astype(jnp.bfloat16)

    return jax.shard_map(local_step, mesh=mesh, in_specs=(row_spec, row_spec, row_spec, row_spec, P("ep"), P("ep"), P("ep")), out_specs=row_spec, check_vma=False)
```

profile of v0, /device:TPU:2, one launch (start us, length us, event | category | flops | bytes accessed | tf_op | source)
XLA Modules:
  0.0 856.2 jit_solution(17965114181939759408)
XLA Ops:
  0.0 0.9 copy.45
  0.9 0.1 eq.42
  1.0 0.1 eq.38
  1.1 0.1 copy.47
  1.2 0.2 fusion.8
  1.5 1.0 select_reduce_fusion
  2.5 0.1 reduce_sum.32
  2.6 0.1 copy.49
  2.7 0.1 reduce_sum.34
  2.8 0.7 broadcast_compare_fusion
  3.5 0.1 copy.54
  3.6 4.2 fusion
  7.8 9.1 %convolution_convert_fusion = bf16[4096,2048]{1,0:T(8,128)(2,1)} fusion(pred[4096,64]{0,1:T(8,128)(4,1)S(1)} %fusion, bf16[64,2048]{1,0:T(8,128)(2,1)} %param.7), kind=kOutput, calls=%fused_computation.3 | convolution fusion | flops 1082130432 | bytes 17301504 | tf_op jit(solution)/shard_map/dot_general | solution.py:37
  16.9 224.0 %all_to_all.8 = bf16[128,1,32,2048]{3,2,1,0:T(8,128)(2,1)S(1)} all-to-all(bf16[128,1,32,2048]{3,2,1,0:T(8,128)(2,1)} %bitcast.47), channel_id=1, replica_groups=mesh['dp'=1,'ep'=128] {'ep'}, dimensions={0} | all-to-all | bytes 33554432 | tf_op jit(solution)/shard_map/all_to_all | solution.py:39
  240.8 5.7 copy-done.2
  246.6 16.6 %fusion.4 = f32[4096,768]{1,0:T(8,128)} fusion(bf16[4096,2048]{1,0:T(8,128)(2,1)S(1)} %bitcast.49, bf16[1,2048,768]{2,1,0:T(8,128)(2,1)S(1)} %copy-done.5), kind=kOutput, calls=%fused_computation.10 | convolution fusion | flops 12884901888 | bytes 32505856 | tf_op jit(solution)/shard_map/erd,edf->erf/dot_general | solution.py:19
  263.2 36.5 %convert_bitcast_fusion = bf16[1,1,4096,2048]{3,2,1,0:T(8,128)(2,1)} fusion(f32[4096,768]{1,0:T(8,128)} %fusion.4, bf16[4096,2048]{1,0:T(8,128)(2,1)} %bitcast.50, bf16[1,768,2048]{2,1,0:T(8,128)(2,1)S(1)} %copy-done, bf16[1,2048,768]{2,1,0:T(8,128)(2,1)} %param.12), kind=kOutput, calls=%fused_computation.2 | convolution fusion | flops 25797066752 | bytes 52428800 | tf_op jit(solution)/shard_map/erf,efd->erd/dot_general | solution.py:22
  299.7 29.2 %copy.62 = bf16[1,1,4096,2048]{3,1,0,2:T(2,128)(2,1)} copy(bf16[1,1,4096,2048]{3,2,1,0:T(8,128)(2,1)} %convert_bitcast_fusion) | data formatting | bytes 33554432 | tf_op jit(solution)/shard_map/reshape | solution.py:41
  328.9 0.5 broadcast.50
  329.4 99.6 %reduce = bf16[4096,2048]{1,0:T(8,128)(2,1)} reduce(bf16[4096,1,1,2048]{3,2,1,0:T(2,128)(2,1)} %bitcast.45, bf16[]{:T(256)} %broadcast.50), dimensions={1,2}, to_apply=%bitcast.41.reduce_sub_computation | reduce | bytes 33554432
  429.0 27.7 %reshape.103 = bf16[128,2,32768]{2,1,0:T(2,128)(2,1)} reshape(bf16[4096,2048]{1,0:T(8,128)(2,1)} %reduce) | data formatting | bytes 33554432
  456.7 32.3 %all-to-all-start.1 = ((bf16[128,2,32768]{2,1,0:T(2,128)(2,1)}), bf16[128,2,32768]{2,1,0:T(2,128)(2,1)}, u32[]{:S(2)}, u32[]{:S(2)}) async-start(bf16[128,2,32768]{2,1,0:T(2,128)(2,1)} %reshape.103), calls=%async_computation.1 | async-start | bytes 33554432 | tf_op jit(solution)/shard_map/all_to_all | solution.py:41
  489.0 0.1 copy.57
  489.1 0.1 reshape.95
  489.2 0.1 copy.52
  489.3 0.1 copy.53
  489.4 248.9 %all-to-all-done.1 = bf16[128,2,32768]{2,1,0:T(2,128)(2,1)} async-done(((bf16[128,2,32768]{2,1,0:T(2,128)(2,1)}), bf16[128,2,32768]{2,1,0:T(2,128)(2,1)}, u32[]{:S(2)}, u32[]{:S(2)}) %all-to-all-start.1) | async-done | bytes 16777248 | tf_op jit(solution)/shard_map/all_to_all | solution.py:41
  738.4 75.6 %reshape.104 = bf16[4096,1,1,2048]{3,2,1,0:T(2,128)(2,1)} reshape(bf16[128,2,32768]{2,1,0:T(2,128)(2,1)} %all-to-all-done.1) | data formatting | bytes 33554432
  814.0 24.2 %copy.61 = bf16[1,1,4096,2048]{3,2,0,1:T(8,128)(2,1)} copy(bf16[1,1,4096,2048]{3,1,0,2:T(2,128)(2,1)} %bitcast.46) | data formatting | bytes 33554432
  838.2 13.3 %gather_fusion = bf16[512,2048]{1,0:T(8,128)(2,1)} fusion(bf16[4096,2048]{1,0:T(8,128)(2,1)} %bitcast.48, s32[1024]{0:T(1024)S(1)} %pad_clamp_fusion), kind=kCustom, calls=%fused_computation | custom fusion | bytes 4196352 | tf_op jit(solution)/shard_map/jit(_take)/gather | solution.py:42
  851.5 4.0 multiply_reduce_fusion
  855.4 0.8 add_convert_fusion
  (21 shorter events, 0.2 us)
Async XLA Ops:
  0.0 263.2 %copy-start = (bf16[1,768,2048]{2,1,0:T(8,128)(2,1)S(1)}, bf16[1,768,2048]{2,1,0:T(8,128)(2,1)}, u32[]{:S(2)}) copy-start(bf16[1,768,2048]{2,1,0:T(8,128)(2,1)} %param.13) | copy-start | bytes 9437188
  16.9 229.7 %copy-start.5 = (bf16[1,2048,768]{2,1,0:T(8,128)(2,1)S(1)}, bf16[1,2048,768]{2,1,0:T(8,128)(2,1)}, u32[]{:S(2)}) copy-start(bf16[1,2048,768]{2,1,0:T(8,128)(2,1)} %param.11) | copy-start | bytes 9437188
  240.8 5.7 copy-start.2
  456.7 32.5 %copy-start.4 = (f32[64,8]{0,1:T(8,128)S(1)}, f32[64,8]{0,1:T(8,128)}, u32[]{:S(2)}) copy-start(f32[64,8]{0,1:T(8,128)} %param.9) | copy-start | bytes 6148
  456.7 281.7 %all-to-all-start.1 = ((bf16[128,2,32768]{2,1,0:T(2,128)(2,1)}), bf16[128,2,32768]{2,1,0:T(2,128)(2,1)}, u32[]{:S(2)}, u32[]{:S(2)}) async-start(bf16[128,2,32768]{2,1,0:T(2,128)(2,1)} %reshape.103), calls=%async_computation.1 | async-start | bytes 33554432 | tf_op jit(solution)/shard_map/all_to_all | solution.py:41
  814.0 42.3 %copy-start.1 = (bf16[1,768,2048]{2,1,0:T(8,128)(2,1)S(1)}, bf16[1,768,2048]{2,1,0:T(8,128)(2,1)}, u32[]{:S(2)}) copy-start(bf16[1,768,2048]{2,1,0:T(8,128)(2,1)} %param.13) | copy-start | bytes 9437188
  838.2 17.2 %copy-start.3 = (bf16[64,2048]{1,0:T(8,128)(2,1)S(1)}, bf16[64,2048]{1,0:T(8,128)(2,1)}, u32[]{:S(2)}) copy-start(bf16[64,2048]{1,0:T(8,128)(2,1)} %param.7) | copy-start | bytes 786436
where the time goes:
time: 859 us; the launch traced here: 856 us
  waiting for transfers between devices  249 us (29%)
  blocking collectives  224 us (26%)
  local copies, waits for them, and re-layouts  178 us (21%)
  other arithmetic  110 us (13%)
  matrix products  62.2 us (7%)
  starting transfers between devices  32.3 us (4%)
    all_to_all x1, waiting for transfers between devices, local_step(): lax.all_to_all(expert_out.reshape(1, n_local, group_size * cap_rows, mode...  249 us
    all_to_all x1, blocking collectives, local_step(): arrived = lax.all_to_all(packed, 'ep', 0, 2, tiled=True)  224 us
    unnamed x18, local copies, waits for them, and re-layouts  135 us
    unnamed x1, other arithmetic  99.6 us
    dot_general x1, matrix products, expert_ffn(): jnp.einsum('erf,efd->erd', hidden, w_down, preferred_element_type=jnp.flo...  36.5 us
    all_to_all x1, starting transfers between devices, local_step(): lax.all_to_all(expert_out.reshape(1, n_local, group_size * cap_rows, mode...  32.3 us
    reshape x1, local copies, waits for them, and re-layouts, local_step(): expert_out.reshape(1, n_local, group_size * cap_rows, model_dim)  29.2 us
  transfers between devices with their start and end apart: 1, of which 1 were waited for; matrix products, arithmetic and copies ran while one was open for 0% of the time, Pallas kernels for 0%

commit v1 on v0

v1 whole, which is shorter than its diff:
```python
import functools

import jax
import jax.numpy as jnp
from jax import lax
from jax.experimental import pallas as pl
from jax.experimental.pallas import tpu as pltpu
from jax.sharding import PartitionSpec as P

MESH = pl.DeviceIdType.MESH
VMEM = pltpu.VMEM
ANY = pl.ANY
GRP = 8
PLN = 16
CAP_C = 32
CAP_R = 48
CH_R, CH_C = 128, 256
K = 72
D = 7
T = K + 3 * D
N_RING = K + 2 * D
N_SEM = 32
INJ = 12


def place_rows(expert_ids, counts_row, cap_rows, n_exp):
    tok_n, top_n = expert_ids.shape
    flat_ids = expert_ids.reshape(tok_n * top_n)
    onehot = (flat_ids[:, None] == jnp.arange(n_exp)[None, :]).astype(jnp.int32)
    before = jnp.cumsum(onehot, axis=0) - onehot
    slot_idx = jnp.sum(before * onehot, axis=1)
    row_limit = jnp.sum(onehot * counts_row[None, :], axis=1)
    buf_pos = jnp.where(slot_idx < row_limit, flat_ids * cap_rows + slot_idx, -1)
    return buf_pos.reshape(tok_n, top_n)


def expert_ffn(rows_in, w_gate, w_up, w_down):
    act_a = jnp.einsum("erd,edf->erf", rows_in, w_gate, preferred_element_type=jnp.float32)
    act_b = jnp.einsum("erd,edf->erf", rows_in, w_up, preferred_element_type=jnp.float32)
    hidden = (jax.nn.silu(act_a) * act_b).astype(jnp.bfloat16)
    return jnp.einsum("erf,efd->erd", hidden, w_down, preferred_element_type=jnp.float32).astype(jnp.bfloat16)


def dense_step(group_size, tokens, expert_ids, gate_w, route_counts, w_gate, w_up, w_down):
    tok_n = expert_ids.shape[0]
    n_local = w_gate.shape[0]
    model_dim = w_gate.shape[1]
    n_exp = n_local * group_size
    cap_rows = tok_n // 2
    buf_pos = place_rows(expert_ids, route_counts[0], cap_rows, n_exp)
    disp_mat = jnp.any(jnp.arange(n_exp * cap_rows)[:, None, None] == buf_pos[None, :, :], axis=2).astype(jnp.bfloat16)
    packed = jnp.dot(disp_mat, tokens, preferred_element_type=jnp.float32).astype(jnp.bfloat16)
    packed = packed.reshape(group_size, n_local, cap_rows, model_dim)
    arrived = lax.all_to_all(packed, "ep", 0, 2, tiled=True)
    expert_out = expert_ffn(arrived.reshape(n_local, group_size * cap_rows, model_dim), w_gate, w_up, w_down)
    returned = lax.all_to_all(expert_out.reshape(1, n_local, group_size * cap_rows, model_dim), "ep", 2, 0, tiled=True)
    picked = jnp.take(returned.reshape(n_exp * cap_rows, model_dim), jnp.maximum(buf_pos, 0), axis=0)
    weights = jnp.where(buf_pos >= 0, gate_w, 0.0)
    total_f32 = tokens.astype(jnp.float32) + jnp.sum(weights[:, :, None] * picked.astype(jnp.float32), axis=1)
    return total_f32.astype(jnp.bfloat16)


def chunk_of(wg, wu, wd, half, k):
    if k < 48:
        arr = wg if k < 24 else wu
        row, col = (k % 24) // 3, (k % 24) % 3
        start = half * 1024 + row * CH_R
    else:
        arr = wd
        row, col = (k - 48) // 8, (k - 48) % 8
        start = half * 384 + row * CH_R
    return arr.at[pl.ds(pl.multiple_of(start, CH_R), CH_R), pl.ds(col * CH_C, CH_C)]


def remote(src, dst, send, recv, dev):
    return pltpu.make_async_remote_copy(
        src_ref=src, dst_ref=dst, send_sem=send, recv_sem=recv, device_id={"ep": dev}, device_id_type=MESH
    )


def drain(ref, sem):
    pltpu.make_async_copy(ref, ref, sem).wait()


def spread_kernel(tok, ids, cnt, wg, wu, wd, tok_all, ids_all, cnt_all, st, xr, own, inj, stage, recv,
                  flags, tok_s, tok_r, ids_s, ids_r, cnt_s, cnt_r, loc, own_sem, inj_s, inj_r, ring_s, ring_r, par_s, par_r, st_sem):
    me = lax.axis_index("ep")
    grp, pos = me // GRP, me % GRP
    core, xx = pos % 2, pos // 2
    other = 1 - core
    partner = grp * GRP + xx * 2 + other
    nbr = grp * GRP + ((xx + 1 + 2 * core) % 4) * 2 + core
    wg, wu, wd = wg.at[0], wu.at[0], wd.at[0]

    loads = [pltpu.make_async_copy(chunk_of(wg, wu, wd, core, k), own.at[k], own_sem) for k in range(K)]
    for cp in loads:
        cp.start()
    bar = pltpu.get_barrier_semaphore()
    for k in range(1, GRP):
        pl.semaphore_signal(bar, inc=1, device_id={"ep": grp * GRP + (pos + k) % GRP}, device_id_type=MESH)
    for k in range(1, PLN):
        pl.semaphore_signal(bar, inc=1, device_id={"ep": ((grp + k) % PLN) * GRP + pos}, device_id_type=MESH)
    pl.semaphore_wait(bar, GRP - 1 + PLN - 1)

    for k in range(1, GRP):
        remote(cnt, cnt_all.at[pos], cnt_s, cnt_r, grp * GRP + (pos + k) % GRP).start()
    pltpu.make_async_copy(cnt, cnt_all.at[pos], loc.at[0]).start()
    for k in range(K):
        remote(chunk_of(wg, wu, wd, other, k), inj.at[k], inj_s, inj_r.at[k // INJ], partner).start()
    for k in range(1, PLN):
        dev = ((grp + k) % PLN) * GRP + pos
        remote(ids, ids_all.at[grp], ids_s, ids_r, dev).start()
        remote(tok, tok_all.at[grp], tok_s, tok_r, dev).start()
    pltpu.make_async_copy(ids, ids_all.at[grp], loc.at[1]).start()
    pltpu.make_async_copy(tok, tok_all.at[grp], loc.at[2]).start()

    pltpu.make_async_copy(cnt, cnt_all.at[pos], loc.at[0]).wait()
    drain(cnt_all.at[pl.ds(0, GRP - 1)], cnt_r)
    total = jnp.sum(cnt_all[...].astype(jnp.float32), axis=0)
    lane = lax.broadcasted_iota(jnp.int32, (8, 128), 1)
    key = total * 8.0 + (7 - lane % GRP).astype(jnp.float32)
    key = jnp.where(lane // GRP == grp, key, -1.0)
    best = jnp.max(key, axis=1, keepdims=True)
    hit = jnp.where(key == best, 1.0, 0.0)
    mine = jnp.max(jnp.where(lane == me, hit, 0.0), axis=1, keepdims=True)
    theirs = jnp.max(jnp.where(lane == partner, hit, 0.0), axis=1, keepdims=True)
    flags[0] = jnp.broadcast_to(mine, (8, 128))
    flags[1] = jnp.broadcast_to(theirs, (8, 128))
    drain(own, own_sem)

    def flag(i):
        row = flags[i, 0:1, :]
        return jnp.concatenate([row, row], axis=1)

    def send(t, src, ring=True):
        if ring:
            remote(src, recv.at[t], ring_s, ring_r.at[t % N_SEM], nbr).start()
        remote(src, xr.at[t], par_s, par_r, partner).start()
        pltpu.make_async_copy(src, st.at[t], st_sem).start()

    def take(t):
        pltpu.make_async_copy(recv.at[t], recv.at[t], ring_r.at[t % N_SEM]).wait()

    def build(t, first):
        a = own[t].astype(jnp.float32)
        b = inj[t].astype(jnp.float32)
        if not first:
            b = jnp.where(flag(1) > 0.5, b, recv[t - D].astype(jnp.float32))
        stage[t] = jnp.where(flag(0) > 0.5, a, b).astype(jnp.bfloat16)

    def head(t, carry):
        build(t, True)
        send(t - 1, stage.at[t - 1])
        return carry

    def body(t, carry):
        take(t - D)
        build(t, False)
        send(t - 1, stage.at[t - 1])
        return carry

    def tail(t, carry):
        take(t - D)
        send(t, recv.at[t - D])
        return carry

    def last(t, carry):
        take(t - D)
        send(t, recv.at[t - D], ring=False)
        return carry

    for blk in range(K // INJ):
        drain(inj.at[pl.ds(blk * INJ, INJ)], inj_r.at[blk])
        lo, hi = blk * INJ, (blk + 1) * INJ
        if blk == 0:
            build(0, True)
            lax.fori_loop(1, D, head, 0)
            lo = D
        lax.fori_loop(lo, hi, body, 0)
    send(K - 1, stage.at[K - 1])
    lax.fori_loop(K, N_RING, tail, 0)
    lax.fori_loop(N_RING, T, last, 0)

    drain(cnt_all.at[pl.ds(0, GRP - 1)], cnt_s)
    drain(inj, inj_s)
    drain(recv, ring_s)
    drain(st, st_sem)
    drain(xr, par_s)
    drain(xr, par_r)
    pltpu.make_async_copy(ids, ids_all.at[grp], loc.at[1]).wait()
    pltpu.make_async_copy(tok, tok_all.at[grp], loc.at[2]).wait()
    drain(ids_all.at[pl.ds(0, PLN - 1)], ids_s)
    drain(ids_all.at[pl.ds(0, PLN - 1)], ids_r)
    drain(tok_all.at[pl.ds(0, PLN - 1)], tok_s)
    drain(tok_all.at[pl.ds(0, PLN - 1)], tok_r)


def spread(tokens, ids_t, cnt_t, w_gate, w_up, w_down):
    dma = pltpu.SemaphoreType.DMA
    bf = jnp.bfloat16
    vm, an = pl.BlockSpec(memory_space=VMEM), pl.BlockSpec(memory_space=ANY)
    return pl.pallas_call(
        spread_kernel,
        out_shape=(
            jax.ShapeDtypeStruct((PLN, 64, 2048), bf),
            jax.ShapeDtypeStruct((PLN, 8, 128), jnp.int32),
            jax.ShapeDtypeStruct((GRP, 8, 128), jnp.int32),
            jax.ShapeDtypeStruct((T, CH_R, CH_C), bf),
            jax.ShapeDtypeStruct((T, CH_R, CH_C), bf),
        ),
        in_specs=[vm, vm, vm, an, an, an],
        out_specs=(an, vm, vm, an, an),
        scratch_shapes=[
            VMEM((K, CH_R, CH_C), bf),
            VMEM((K, CH_R, CH_C), bf),
            VMEM((K, CH_R, CH_C), bf),
            VMEM((N_RING, CH_R, CH_C), bf),
            VMEM((2, 8, 128), jnp.float32),
            dma, dma, dma, dma, dma, dma, dma((3,)), dma, dma, dma((K // INJ,)), dma, dma((N_SEM,)), dma, dma, dma,
        ],
        compiler_params=pltpu.CompilerParams(collective_id=0, has_side_effects=True, vmem_limit_bytes=48 * 2**20),
    )(tokens, ids_t, cnt_t, w_gate, w_up, w_down)


def swap_kernel(n, dev_of, my_of, rows, flg, out, flg_out, row_s, row_r, flg_s, flg_r, loc):
    me = lax.axis_index("ep")
    mine = my_of(me)
    bar = pltpu.get_barrier_semaphore()
    for k in range(1, n):
        pl.semaphore_signal(bar, inc=1, device_id={"ep": dev_of(me, (mine + k) % n)}, device_id_type=MESH)
    here = pltpu.make_async_copy(rows.at[mine], out.at[mine], loc.at[0])
    here_f = pltpu.make_async_copy(flg, flg_out.at[mine], loc.at[1])
    here.start()
    here_f.start()
    pl.semaphore_wait(bar, n - 1)
    for k in range(1, n):
        peer = (mine + k) % n
        dev = dev_of(me, peer)
        remote(rows.at[peer], out.at[mine], row_s, row_r, dev).start()
        remote(flg, flg_out.at[mine], flg_s, flg_r, dev).start()
    here.wait()
    here_f.wait()
    drain(rows.at[pl.ds(0, n - 1)], row_s)
    drain(out.at[pl.ds(0, n - 1)], row_r)
    drain(flg_out.at[pl.ds(0, n - 1)], flg_s)
    drain(flg_out.at[pl.ds(0, n - 1)], flg_r)


def swap(rows, flg, n, cid):
    if n == GRP:
        dev_of, my_of = (lambda me, i: (me // GRP) * GRP + i), (lambda me: me % GRP)
    else:
        dev_of, my_of = (lambda me, i: i * GRP + me % GRP), (lambda me: me // GRP)
    dma = pltpu.SemaphoreType.DMA
    vm = pl.BlockSpec(memory_space=VMEM)
    return pl.pallas_call(
        functools.partial(swap_kernel, n, dev_of, my_of),
        out_shape=(jax.ShapeDtypeStruct(rows.shape, rows.dtype), jax.ShapeDtypeStruct((n, 8, 128), jnp.int32)),
        in_specs=[vm, vm],
        out_specs=(vm, vm),
        scratch_shapes=[dma, dma, dma, dma, dma((2,))],
        compiler_params=pltpu.CompilerParams(collective_id=cid, has_side_effects=True, vmem_limit_bytes=24 * 2**20),
    )(rows, flg)


def ffn_rows(x, y, wg, wu, wd):
    def block(i, carry):
        at = pl.ds(pl.multiple_of(i * 256, 256), 256)
        rows = x[at, :]
        a = jnp.dot(rows, wg[...], preferred_element_type=jnp.float32)
        b = jnp.dot(rows, wu[...], preferred_element_type=jnp.float32)
        h = (jax.nn.silu(a) * b).astype(jnp.bfloat16)
        y[at, :] = jnp.dot(h, wd[...], preferred_element_type=jnp.float32).astype(jnp.bfloat16)
        return carry

    lax.fori_loop(0, x.shape[0] // 256, block, 0)


def ffn_kernel(info, st, xr, wg, wu, wd, xc, xh, yc, yh, cg, cu, cd, hg, hu, hd, sems):
    wg, wu, wd = wg.at[0], wu.at[0], wd.at[0]
    own = [pltpu.make_async_copy(s, d, sems.at[i]) for i, (s, d) in enumerate(((wg, cg), (wu, cu), (wd, cd)))]
    for cp in own:
        cp.start()
    core, first, second = info[0], info[1], info[2]
    for k in range(K):
        sem = sems.at[3 + k // 24]
        pltpu.make_async_copy(st.at[first + k], chunk_of(hg, hu, hd, core, k), sem).start()
        pltpu.make_async_copy(xr.at[second + k], chunk_of(hg, hu, hd, 1 - core, k), sem).start()
    for cp in own:
        cp.wait()
    ffn_rows(xc, yc, cg, cu, cd)
    for i, (s, d) in enumerate(((wg, hg), (wu, hu), (wd, hd))):
        pltpu.make_async_copy(s, d, sems.at[3 + i]).wait()
    ffn_rows(xh, yh, hg, hu, hd)


def ffn(info, st, xr, w_gate, w_up, w_down, xc, xh):
    bf = jnp.bfloat16
    vm, an = pl.BlockSpec(memory_space=VMEM), pl.BlockSpec(memory_space=ANY)
    up, down = VMEM((2048, 768), bf), VMEM((768, 2048), bf)
    return pl.pallas_call(
        ffn_kernel,
        out_shape=(jax.ShapeDtypeStruct(xc.shape, bf), jax.ShapeDtypeStruct(xh.shape, bf)),
        in_specs=[pl.BlockSpec(memory_space=pltpu.SMEM), an, an, an, an, an, vm, vm],
        out_specs=(vm, vm),
        scratch_shapes=[up, up, down, up, up, down, pltpu.SemaphoreType.DMA((6,))],
        compiler_params=pltpu.CompilerParams(vmem_limit_bytes=48 * 2**20),
    )(info, st, xr, w_gate, w_up, w_down, xc, xh)


def strict_upper(n):
    i = jnp.arange(n)
    return (i[:, None] < i[None, :]).astype(jnp.bfloat16)


def small_dot(a, b):
    return jnp.dot(a.astype(jnp.bfloat16), b, preferred_element_type=jnp.float32)


def flag_tile(ok):
    return jnp.broadcast_to(ok.astype(jnp.int32), (8, 128))


def sparse_step(tokens, expert_ids, gate_w, route_counts, w_gate, w_up, w_down):
    bf, f32 = jnp.bfloat16, jnp.float32
    me = lax.axis_index("ep")
    grp, pos = me // GRP, me % GRP
    core, xx = pos % 2, pos // 2
    ids_t = jnp.pad(expert_ids.T, ((0, 0), (0, 64)))
    cnt_t = jnp.broadcast_to(route_counts, (8, 128))
    tok_all, ids_all, cnt_all, st, xr = spread(tokens, ids_t, cnt_t, w_gate, w_up, w_down)

    e_ar = jnp.arange(128)
    hits = expert_ids[:, :, None] == e_ar[None, None, :]
    named = jnp.any(hits, axis=1)
    gates = jnp.sum(jnp.where(hits, gate_w[:, :, None], 0.0), axis=1)
    slot = jnp.dot(strict_upper(64).T, named.astype(bf), preferred_element_type=f32)
    kept = named & (slot < 32)
    n_kept = jnp.sum(kept.astype(f32), axis=0)
    same = (e_ar[:, None] // GRP) == (e_ar[None, :] // GRP)
    before = small_dot(n_kept[None, :], (same & (e_ar[:, None] < e_ar[None, :])).astype(bf))
    back = jnp.where(kept, before + slot, -1.0).astype(jnp.int32)
    gates = jnp.where(kept, gates, 0.0)
    fits_src = jnp.max(jnp.sum(n_kept.reshape(PLN, GRP), axis=1)) <= CAP_R

    totals = lax.dynamic_slice(jnp.sum(cnt_all[:, 0, :], axis=0), (grp * GRP,), (GRP,))
    hot = jnp.argmax(totals).astype(jnp.int32)
    local_ids = ids_all[:, :, :64] - grp * GRP
    p_ar = jnp.arange(GRP)
    m0 = jnp.any(local_ids[None] == p_ar[:, None, None, None], axis=2)
    q = jnp.dot(m0.astype(bf).reshape(GRP * PLN, 64), strict_upper(64), preferred_element_type=f32).reshape(GRP, PLN, 64)
    m = m0 & (q < 32)
    n_ps = jnp.sum(m.astype(f32), axis=2)
    rank = (small_dot(n_ps, strict_upper(PLN))[:, :, None] + q).astype(jnp.int32)
    back_at = (small_dot(n_ps.T, strict_upper(GRP)).T[:, :, None] + q).astype(jnp.int32)
    is_hot = p_ar == hot
    fits_mid = jnp.all(is_hot | (jnp.sum(n_ps, axis=1) <= CAP_C))
    rank_c = jnp.where(m & ~is_hot[:, None, None], rank, -1).reshape(GRP, 1, PLN * 64)
    rank_h = jnp.max(jnp.where(m & is_hot[:, None, None], rank, -1), axis=0).reshape(1, PLN * 64)
    disp_c = (jnp.arange(CAP_C)[None, :, None] == rank_c).astype(bf).reshape(GRP * CAP_C, PLN * 64)
    disp_h = (jnp.arange(512)[:, None] == rank_h).astype(bf)
    toks = tok_all.reshape(PLN * 64, 2048)
    rows_c = jnp.dot(disp_c, toks, preferred_element_type=f32).astype(bf)
    rows_h = jnp.dot(disp_h, toks, preferred_element_type=f32).astype(bf)

    arrived, ok_grp = swap(rows_c.reshape(GRP, CAP_C, 2048), flag_tile(fits_src & fits_mid), GRP, 1)
    hx = hot // 2
    hops = jnp.where(core == 0, xx - hx, hx - xx) % 4
    info = jnp.stack([core, D * hops, D * ((4 - hops) % 4)]).astype(jnp.int32)
    y_c, y_h = ffn(info, st, xr, w_gate, w_up, w_down, arrived.reshape(GRP * CAP_C, 2048), rows_h)
    ok_tile = jnp.broadcast_to(jnp.min(ok_grp[:, :1, :1]), (8, 128))
    home_c, _ = swap(y_c.reshape(GRP, CAP_C, 2048), ok_tile, GRP, 2)

    row = jnp.where(is_hot[:, None, None], GRP * CAP_C + rank, p_ar[:, None, None] * CAP_C + rank)
    r_ar = jnp.arange(CAP_R)
    pick = jnp.where(m[:, :, None, :] & (back_at[:, :, None, :] == r_ar[None, None, :, None]), row[:, :, None, :] + 1, 0)
    src_row = jnp.sum(pick, axis=(0, 3)) - 1
    pack = (src_row.reshape(PLN * CAP_R, 1) == jnp.arange(GRP * CAP_C + 512)[None, :]).astype(bf)
    y_all = jnp.concatenate([home_c.reshape(GRP * CAP_C, 2048), y_h], axis=0)
    ret = jnp.dot(pack, y_all, preferred_element_type=f32).astype(bf)
    home, ok_all = swap(ret.reshape(PLN, CAP_R, 2048), ok_tile, PLN, 3)

    comb = jnp.sum(
        jnp.where(back.reshape(64, PLN, GRP)[:, :, :, None] == r_ar, gates.reshape(64, PLN, GRP)[:, :, :, None], 0.0), axis=2
    ).reshape(64, PLN * CAP_R)
    g1 = lax.reduce_precision(comb, 8, 7)
    g2 = lax.reduce_precision(comb - g1, 8, 7)
    g3 = lax.reduce_precision(comb - g1 - g2, 8, 7)
    parts = jnp.dot(
        jnp.concatenate([g1, g2, g3], axis=0).astype(bf), home.reshape(PLN * CAP_R, 2048), preferred_element_type=f32
    )
    total = tokens.astype(f32) + (parts[:64] + (parts[64:128] + parts[128:]))
    return total.astype(bf), jnp.min(ok_all[:, 0, 0]) > 0


def solution(mesh):
    group_size = mesh.shape["ep"]
    row_spec = P(("dp", "ep"))

    def local_step(*args):
        fast, ok = sparse_step(*args)
        return lax.cond(ok, lambda: fast, lambda: dense_step(group_size, *args))

    return jax.shard_map(
        local_step,
        mesh=mesh,
        in_specs=(row_spec, row_spec, row_spec, row_spec, P("ep"), P("ep"), P("ep")),
        out_specs=row_spec,
        check_vma=False,
    )
```

time: 859 us -> 236 us (0.27)
  the two profiles are of different devices: /device:TPU:2 before, /device:TPU:7 now
where the time goes in v1:
time: 236 us; the launch traced here: 232 us
  Pallas kernels  192 us (81%)
  matrix products  14.2 us (6%)
  other arithmetic  11.7 us (5%)
  local copies, waits for them, and re-layouts  8.61 us (4%)
  between operations  5.25 us (2%)
    pallas_call x3, Pallas kernels, swap(): pl.pallas_call(functools.partial(swap_kernel, n, dev_of, my_of), out_shap...  102 us
    pallas_call x1, Pallas kernels, spread(): pl.pallas_call(spread_kernel, out_shape=(jax.ShapeDtypeStruct((PLN, 64, 2...  76.2 us
    pallas_call x1, Pallas kernels, ffn(): pl.pallas_call(ffn_kernel, out_shape=(jax.ShapeDtypeStruct(xc.shape, bf),...  13.2 us
    dot_general x1, matrix products, sparse_step(): rows_h = jnp.dot(disp_h, toks, preferred_element_type=f32).astype(bf)  5.84 us

profile of v1, /device:TPU:7, one launch (start us, length us, event | category | flops | bytes accessed | tf_op | source)
XLA Modules:
  0.0 231.6 jit_solution(16036099990840848961)
XLA Ops:
  0.0 0.7 broadcast_in_dim.127.cnt
  0.7 0.7 pad.4.ids
  1.3 76.2 %shard_map.75 = (bf16[16,64,2048]{2,1,0:T(8,128)(2,1)S(1)}, s32[16,8,128]{2,1,0:T(8,128)S(1)}, s32[8,8,128]{2,1,0:T(8,128)S(1)}, bf16[93,128,256]{2,1,0:T(8,128)(2,1)}, bf16[93,128,256]{2,1,0:T(8,128)(2,1)}) custom-call(bf16[64,2048]{1,0:T(8,128)(2,1)} %tok.1, s32[8,128]{1,0:T(8,128)S(1)} %pad.4.ids, s32[8,128]{1,0:T(8,128)S(1)} %broadcast_in_dim.127.cnt, ...), custom_call_target="tpu_custom_call" | custom-call | tf_op jit(solution)/shard_map/pallas_call | solution.py:202
  77.5 1.9 copy-done
  79.9 0.2 fusion.43
  80.3 0.8 iota_reduce_fusion
  81.0 1.3 or_reduce_fusion
  82.5 0.7 fusion.50
  83.3 1.0 select_reduce_fusion.2
  84.4 5.8 %convolution_convert_fusion.2.xh = bf16[512,2048]{1,0:T(8,128)(2,1)} fusion(bf16[1024,2048]{1,0:T(8,128)(2,1)} %bitcast.84, s32[1024]{0:T(1024)S(1)} %eq.202), kind=kOutput, calls=%fused_computation.40 | convolution fusion | flops 2149056512 | bytes 6295552 | tf_op jit(solution)/shard_map/dot_general | solution.py:364
  90.5 3.4 %convolution_convert_fusion.3 = bf16[256,2048]{1,0:T(8,128)(2,1)S(1)} fusion(pred[256,1024]{1,0:T(32,128)(4,1)S(1)} %bitcast.96, bf16[1024,2048]{1,0:T(8,128)(2,1)} %bitcast.85), kind=kOutput, calls=%fused_computation.41 | convolution fusion | flops 1074266112 | bytes 5505024 | tf_op jit(solution)/shard_map/dot_general | solution.py:363
  94.1 0.2 select_reduce_fusion.3
  94.5 0.8 broadcast_select_fusion
  95.5 0.7 reduce_max.18
  97.5 15.3 %shard_map.76 = (bf16[8,32,2048]{2,1,0:T(8,128)(2,1)S(1)}, s32[8,8,128]{2,1,0:T(8,128)S(1)}) custom-call(bf16[8,32,2048]{2,1,0:T(8,128)(2,1)S(1)} %bitcast.81, s32[8,128]{1,0:T(8,128)S(1)} %broadcast_in_dim.132.flg), custom_call_target="tpu_custom_call" | custom-call | tf_op jit(solution)/shard_map/pallas_call | solution.py:256
  115.7 13.2 %shard_map.77 = (bf16[256,2048]{1,0:T(8,128)(2,1)S(1)}, bf16[512,2048]{1,0:T(8,128)(2,1)S(1)}) custom-call(s32[3]{0:T(128)S(1)} %pad_add_fusion.info, bf16[93,128,256]{2,1,0:T(8,128)(2,1)} %get-tuple-element.46.st, bf16[93,128,256]{2,1,0:T(8,128)(2,1)} %get-tuple-element.47.xr, bf16[1,2048,768]{2,1,0:T(8,128)(2,1)} %wg.3, bf16[1,2048,768]{2,1,0:T(8,128)(2,1)} %wu.3, ...), custom_call_target="tpu_custom_call" | custom-call | tf_op jit(solution)/shard_map/pallas_call | solution.py:301
  129.0 0.6 slice_reduce_fusion.1
  129.6 0.6 broadcast_in_dim.133.flg
  130.2 16.4 %shard_map.78 = (bf16[8,32,2048]{2,1,0:T(8,128)(2,1)S(1)}, s32[8,8,128]{2,1,0:T(8,128)}) custom-call(bf16[8,32,2048]{2,1,0:T(8,128)(2,1)S(1)} %bitcast.82, s32[8,128]{1,0:T(8,128)S(1)} %broadcast_in_dim.133.flg), custom_call_target="tpu_custom_call" | custom-call | tf_op jit(solution)/shard_map/pallas_call | solution.py:256
  146.7 2.7 %convolution_convert_fusion.1 = bf16[768,2048]{1,0:T(8,128)(2,1)S(1)} fusion(bf16[512,2048]{1,0:T(8,128)(2,1)S(1)} %get-tuple-element.53, bf16[256,2048]{1,0:T(8,128)(2,1)S(1)} %bitcast.86, s32[768]{0:T(1024)S(1)} %sub.55), kind=kOutput, calls=%fused_computation.31 | convolution fusion | flops 2424373248 | bytes 6294528 | tf_op jit(solution)/shard_map/dot_general | solution.py:380
  149.3 70.4 %shard_map.79 = (bf16[16,48,2048]{2,1,0:T(8,128)(2,1)S(1)}, s32[16,8,128]{2,1,0:T(8,128)S(1)}) custom-call(bf16[16,48,2048]{2,1,0:T(8,128)(2,1)S(1)} %bitcast.80, s32[8,128]{1,0:T(8,128)S(1)} %broadcast_in_dim.133.flg), custom_call_target="tpu_custom_call" | custom-call | tf_op jit(solution)/shard_map/pallas_call | solution.py:256
  219.8 0.2 convolution_bitcast_fusion
  220.0 0.6 select_convert_fusion
  220.6 0.8 copy.54
  221.5 1.5 copy.56
  223.0 2.2 select_reduce_fusion.1
  225.2 1.8 copy.60
  227.0 1.0 reduce-precision_convert_fusion.1
  228.0 0.8 fusion.22
  228.8 0.8 fusion.20
  229.6 0.7 slice_reduce_fusion
  231.1 0.2 conditional.1
  (34 shorter events, 1.9 us)
Async XLA Ops:
  77.5 1.9 copy-start
  90.2 3.7 %copy-start.6 = (s32[64,8]{0,1:T(8,128)S(1)}, s32[64,8]{0,1:T(8,128)}, u32[]{:S(2)}) copy-start(s32[64,8]{0,1:T(8,128)} %param.10) | copy-start | bytes 6148
  90.2 3.8 %copy-start.8 = (f32[64,8]{0,1:T(8,128)S(1)}, f32[64,8]{0,1:T(8,128)}, u32[]{:S(2)}) copy-start(f32[64,8]{0,1:T(8,128)} %param.11) | copy-start | bytes 6148
  219.8 9.1 %copy-start.3 = (bf16[64,2048]{1,0:T(8,128)(2,1)S(1)}, bf16[64,2048]{1,0:T(8,128)(2,1)}, u32[]{:S(2)}) copy-start(bf16[64,2048]{1,0:T(8,128)(2,1)} %tok.1) | copy-start | bytes 786436
  225.2 5.9 %copy-start.9 = (f32[64,8]{0,1:T(8,128)S(1)}, f32[64,8]{0,1:T(8,128)}, u32[]{:S(2)}) copy-start(f32[64,8]{0,1:T(8,128)} %param.11) | copy-start | bytes 6148
  225.2 5.9 %copy-start.10 = (s32[1,128]{1,0:T(1,128)S(1)}, s32[1,128]{1,0:T(1,128)}, u32[]{:S(2)}) copy-start(s32[1,128]{1,0:T(1,128)} %param.12) | copy-start | bytes 1540

commit v2 on v0

v2 whole, which is shorter than its diff:
```python
import functools

import jax
import jax.numpy as jnp
from jax import lax
from jax.experimental import pallas as pl
from jax.experimental.pallas import tpu as pltpu
from jax.sharding import PartitionSpec as P

MESH = pl.DeviceIdType.MESH
VMEM = pltpu.VMEM
ANY = pl.ANY
F32 = jnp.float32
MODEL, FFN, TILE, MIB = 2048, 768, (8, 128), 2**20
DOWN, ACROSS = dict(axis=0, keepdims=True), dict(axis=1, keepdims=True)
EFFECTS = dict(has_side_effects=True)
GRP = 8
PLN = 16
CAP_C = 32
CH_R, CH_C = 128, 256
K = 72
D = 7
T = K + 3 * D
N_RING = K + 2 * D
N_SEM = 32
INJ = 12
CAP_B = 16
RING_AG = 44
RING_X1, RING_X2 = 8, 12
FAR = (10, 6, 14, 9, 11, 2, 8, 5, 7, 13, 15, 1, 3, 4, 12)


def place_rows(expert_ids, counts_row, cap_rows, n_exp):
    tok_n, top_n = expert_ids.shape
    flat_ids = expert_ids.reshape(tok_n * top_n)
    onehot = (flat_ids[:, None] == jnp.arange(n_exp)[None, :]).astype(jnp.int32)
    before = jnp.cumsum(onehot, axis=0) - onehot
    slot_idx = jnp.sum(before * onehot, axis=1)
    row_limit = jnp.sum(onehot * counts_row[None, :], axis=1)
    buf_pos = jnp.where(slot_idx < row_limit, flat_ids * cap_rows + slot_idx, -1)
    return buf_pos.reshape(tok_n, top_n)


def expert_ffn(rows_in, w_gate, w_up, w_down):
    act_a = jnp.einsum("erd,edf->erf", rows_in, w_gate, preferred_element_type=F32)
    act_b = jnp.einsum("erd,edf->erf", rows_in, w_up, preferred_element_type=F32)
    hidden = (jax.nn.silu(act_a) * act_b).astype(jnp.bfloat16)
    return jnp.einsum("erf,efd->erd", hidden, w_down, preferred_element_type=F32).astype(jnp.bfloat16)


def dense_step(group_size, tokens, expert_ids, gate_w, route_counts, w_gate, w_up, w_down):
    tok_n = expert_ids.shape[0]
    n_local = w_gate.shape[0]
    model_dim = w_gate.shape[1]
    n_exp = n_local * group_size
    cap_rows = tok_n // 2
    buf_pos = place_rows(expert_ids, route_counts[0], cap_rows, n_exp)
    disp_mat = jnp.any(jnp.arange(n_exp * cap_rows)[:, None, None] == buf_pos[None, :, :], axis=2).astype(jnp.bfloat16)
    packed = jnp.dot(disp_mat, tokens, preferred_element_type=F32).astype(jnp.bfloat16)
    packed = packed.reshape(group_size, n_local, cap_rows, model_dim)
    arrived = lax.all_to_all(packed, "ep", 0, 2, tiled=True)
    expert_out = expert_ffn(arrived.reshape(n_local, group_size * cap_rows, model_dim), w_gate, w_up, w_down)
    returned = lax.all_to_all(expert_out.reshape(1, n_local, group_size * cap_rows, model_dim), "ep", 2, 0, tiled=True)
    picked = jnp.take(returned.reshape(n_exp * cap_rows, model_dim), jnp.maximum(buf_pos, 0), axis=0)
    weights = jnp.where(buf_pos >= 0, gate_w, 0.0)
    total_f32 = tokens.astype(jnp.float32) + jnp.sum(weights[:, :, None] * picked.astype(jnp.float32), axis=1)
    return total_f32.astype(jnp.bfloat16)


def chunk_of(wg, wu, wd, half, k):
    if k < 48:
        arr = wg if k < 24 else wu
        row, col = (k % 24) // 3, (k % 24) % 3
        start = half * 1024 + row * CH_R
    else:
        arr = wd
        row, col = (k - 48) // 8, (k - 48) % 8
        start = half * 384 + row * CH_R
    return arr.at[pl.ds(pl.multiple_of(start, CH_R), CH_R), pl.ds(col * CH_C, CH_C)]


def remote(src, dst, send, recv, dev):
    return pltpu.make_async_remote_copy(
        src_ref=src, dst_ref=dst, send_sem=send, recv_sem=recv, device_id={"ep": dev}, device_id_type=MESH
    )


def block_at(i, n):
    return pl.ds(i * n if isinstance(i, int) else pl.multiple_of(i * n, n), n)


def first(n):
    return pl.ds(0, n)


def others(ref):
    return ref.at[first(ref.shape[0] - 1)]


def plane_peer(grp, k):
    return ((grp // 4 + k // 4) % 4) * 4 + (grp % 4 + k % 4) % 4


def drain(ref, sem):
    pltpu.make_async_copy(ref, ref, sem).wait()


def ffn_rows(x, y, wg, wu, wd):
    def block(i, carry):
        at = block_at(i, 256)
        rows = x[at, :]
        a = jnp.dot(rows, wg[...], preferred_element_type=F32)
        b = jnp.dot(rows, wu[...], preferred_element_type=F32)
        h = (jax.nn.silu(a) * b).astype(jnp.bfloat16)
        y[at, :] = jnp.dot(h, wd[...], preferred_element_type=F32).astype(jnp.bfloat16)
        return carry

    lax.fori_loop(0, x.shape[0] // 256, block, 0)


def iota(shape, dim):
    return lax.broadcasted_iota(jnp.int32, shape, dim)


def ones_where(cond):
    return jnp.where(cond, 1.0, 0.0).astype(jnp.bfloat16)


def fdot(a, b):
    return jnp.dot(a.astype(jnp.bfloat16), b.astype(jnp.bfloat16), preferred_element_type=F32)


def main_kernel(tok, ids, gat, cnt, wg, wu, wd,
                rows_h, st, xr, cold_home, gh, gc, ok_all, info,
                own, inj, stage, recv, cg, cu, cd, toks, rows_c, arr, y_c, home_c, ret_c, hid,
                sl, gt, tab_all, cnt_all, hot_all, flags, hot_t, ok_t, ok_grp, rk, kc, sh, disp, kexp, pack, ght, gct,
                dma1, inj_r, ring_r):
    me = lax.axis_index("ep")
    grp, pos = me // GRP, me % GRP
    zz, yy = grp // 4, grp % 4
    core, xx = pos % 2, pos // 2
    other = 1 - core
    partner = grp * GRP + xx * 2 + other
    nbr = grp * GRP + ((xx + 1 + 2 * core) % 4) * 2 + core
    wg, wu, wd = wg.at[0], wu.at[0], wd.at[0]
    (own_sem, w0_sem, w1_sem, w2_sem, cnt_s, cnt_r, tab_s, tab_r, hot_s, hot_r, inj_s, a1_s, a1_r, b1_s, b1_r, p2_s, p2_r,
     xd_s, xd_r, ok_s, ok_r, xb_s, xb_r, pr_s, pr_r, oa_s, oa_r, ring_s, par_s, par_r, st_sem, loc_sem) = [dma1.at[i] for i in range(32)]

    def xdev(k):
        return grp * GRP + (pos + k) % GRP

    def pdev(k):
        return ((grp + k) % PLN) * GRP + pos

    for k in range(K):
        pltpu.make_async_copy(chunk_of(wg, wu, wd, core, k), own.at[k], own_sem).start()
    mine_at = block_at(grp, 64)
    pltpu.make_async_copy(tok, toks.at[mine_at], loc_sem).start()
    full = [pltpu.make_async_copy(s, d, q) for s, d, q in ((wg, cg, w0_sem), (wu, cu, w1_sem), (wd, cd, w2_sem))]

    sq = (128, 128)
    e_i = iota(sq, 0)
    named = jnp.zeros(sq, F32)
    gates = jnp.zeros(sq, F32)
    for j in range(8):
        hit_j = ids[j : j + 1, :] == e_i
        named = jnp.where(hit_j, 1.0, named)
        gates = jnp.where(hit_j, gat[j : j + 1, :], gates)
    l0, l1 = iota(sq, 0), iota(sq, 1)
    slot = fdot(named, ones_where(((l0 >> 6) == (l1 >> 6)) & (l0 < l1)))
    sl[...] = jnp.where((named > 0.5) & (slot < 32.0), slot, -1.0).reshape(PLN, *TILE)
    gt[...] = gates.reshape(PLN, *TILE)

    bar = pltpu.get_barrier_semaphore()
    for k in range(1, GRP):
        pl.semaphore_signal(bar, inc=1, device_id={"ep": xdev(k)}, device_id_type=MESH)
    for k in range(1, PLN):
        pl.semaphore_signal(bar, inc=1, device_id={"ep": pdev(k)}, device_id_type=MESH)
    pl.semaphore_wait(bar, GRP - 1 + PLN - 1)

    for k in range(1, GRP):
        remote(cnt, cnt_all.at[pos], cnt_s, cnt_r, xdev(k)).start()
    cnt_all[pos] = cnt[...]

    def half_at(z, y, h):
        return pl.ds(pl.multiple_of(((z % 4) * 4 + (y % 4)) * 64 + 32 * h, 32), 32)

    def plane_dev(z, y):
        return ((z % 4) * 4 + (y % 4)) * GRP + pos

    for k in (1, 3, 2):
        remote(tok.at[first(32)], toks.at[half_at(zz, yy, 0)], a1_s, a1_r, plane_dev(zz, yy + k)).start()
        remote(tok.at[pl.ds(32, 32)], toks.at[half_at(zz, yy, 1)], b1_s, b1_r, plane_dev(zz + k, yy)).start()
    for k in range(K):
        remote(chunk_of(wg, wu, wd, other, k), inj.at[k], inj_s, inj_r.at[k // INJ], partner).start()
    for k in range(1, PLN):
        remote(sl.at[(grp + k) % PLN], tab_all.at[grp], tab_s, tab_r, pdev(k)).start()
    tab_all[grp] = sl[grp]
    for cp in full:
        cp.start()

    drain(others(cnt_all), cnt_r)
    total = jnp.sum(cnt_all[...].astype(jnp.float32), axis=0)
    lane = iota(TILE, 1)
    key = total * 8.0 + (7 - (lane & 7)).astype(jnp.float32)
    key = jnp.where((lane >> 3) == grp, key, -1.0)
    best = jnp.max(key, **ACROSS)
    hit = jnp.where(key == best, 1.0, 0.0)
    mine = jnp.max(jnp.where(lane == me, hit, 0.0), **ACROSS)
    theirs = jnp.max(jnp.where(lane == partner, hit, 0.0), **ACROSS)
    flags[0] = jnp.broadcast_to(mine, TILE)
    flags[1] = jnp.broadcast_to(theirs, TILE)
    hot_p = jnp.max(jnp.where(lane == grp * 8 + iota(TILE, 0), hit, 0.0), **ACROSS)
    hot_t[...] = jnp.broadcast_to(hot_p, TILE)
    hx = jnp.sum(hit * ((lane & 7) >> 1).astype(jnp.float32), **ACROSS).astype(jnp.int32)
    sign = 1 - 2 * core
    hops = (sign * (xx - hx) + 8) & 3
    info[...] = jnp.where(iota(TILE, 0) == 0, D * hops, D * ((4 - hops) & 3))
    drain(own, own_sem)

    def flag(i):
        row = flags[i, 0:1, :]
        return jnp.concatenate([row, row], axis=1)

    def send(t, src, ring=True):
        if ring:
            remote(src, recv.at[t], ring_s, ring_r.at[t % N_SEM], nbr).start()
        remote(src, xr.at[t], par_s, par_r, partner).start()
        pltpu.make_async_copy(src, st.at[t], st_sem).start()

    def take(t):
        pltpu.make_async_copy(recv.at[t], recv.at[t], ring_r.at[t % N_SEM]).wait()

    def build(t, first):
        a = own[t].astype(jnp.float32)
        b = inj[t].astype(jnp.float32)
        if not first:
            b = jnp.where(flag(1) > 0.5, b, recv[t - D].astype(jnp.float32))
        stage[t] = jnp.where(flag(0) > 0.5, a, b).astype(jnp.bfloat16)

    def head(t):
        build(t, True)
        send(t - 1, stage.at[t - 1])

    def body(t):
        take(t - D)
        build(t, False)
        send(t - 1, stage.at[t - 1])

    def tail(t):
        take(t - D)
        send(t, recv.at[t - D])

    def last(t):
        take(t - D)
        send(t, recv.at[t - D], ring=False)

    at = [0]

    def ring(n, task=None):
        base = at[0]
        end = min(base + n, T)
        while at[0] < end:
            t = at[0]
            if t < K and t % INJ == 0:
                drain(inj.at[pl.ds(t, INJ)], inj_r.at[t // INJ])
            if t == K:
                send(K - 1, stage.at[K - 1])
            if t == 0:
                build(0, True)
                if task is not None:
                    task(0)
                at[0] = 1
                continue
            kind, stop = (head, D) if t < D else (body, (t // INJ + 1) * INJ) if t < K else (tail, N_RING) if t < N_RING else (last, T)
            stop = min(stop, end)

            def step(i, carry, kind=kind):
                kind(i)
                if task is not None:
                    task(i - base)
                return carry

            lax.fori_loop(t, stop, step, 0)
            at[0] = stop
        if task is not None:
            for i in range(end - base, n):
                task(i)

    ring(1)
    for k in range(1, PLN):
        remote(hot_t, hot_all.at[grp], hot_s, hot_r, pdev(k)).start()
    hot_all[grp] = hot_t[...]
    ring(3)
    pltpu.make_async_copy(tok, toks.at[mine_at], loc_sem).wait()
    drain(toks.at[first(96)], a1_r)
    drain(toks.at[first(96)], b1_r)
    for k in (2, 1, 3):
        for i in range(4):
            a_at, b_at = half_at(zz, yy + i, 0), half_at(zz + i, yy, 1)
            remote(toks.at[a_at], toks.at[a_at], p2_s, p2_r, plane_dev(zz + k, yy)).start()
            remote(toks.at[b_at], toks.at[b_at], p2_s, p2_r, plane_dev(zz, yy + k)).start()

    ring(3)
    drain(others(hot_all), hot_r)

    def gate_task(g):
        s, w, h = sl[g], gt[g], hot_all[g]
        s_h = jnp.sum(h * (s + 1.0), **DOWN) - 1.0
        w_h = jnp.sum(h * w, **DOWN)
        ght[block_at(g, 32), :] = jnp.where(iota((32, 128), 0).astype(jnp.float32) == s_h, w_h, 0.0)
        n = jnp.sum(jnp.where((s >= 0.0) & (lane < 64), 1.0 - h, 0.0), **ACROSS)
        off = jnp.zeros((1, 1), jnp.float32)
        acc = jnp.zeros((16, 128), jnp.float32)
        r_i = iota((16, 128), 0).astype(jnp.float32)
        for p in range(GRP):
            s_p = s[p : p + 1, :]
            use = (s_p >= 0.0) & (h[p : p + 1, :] < 0.5)
            r_p = jnp.where(use, s_p + off, -1.0)
            acc = acc + jnp.where(r_i == r_p, w[p : p + 1, :], 0.0)
            off = off + n[p : p + 1, :]
        gct[block_at(g, 16), :] = acc

    ring(16, gate_task)
    gh[...] = ght[...].T
    gc[...] = gct[...].T
    ring(1)

    drain(others(tab_all), tab_r)
    hot16 = jnp.concatenate([hot_t[:, 0:1], jnp.zeros((8, 1), jnp.float32)], axis=0)
    s8 = jnp.concatenate([jnp.where(lane < 64, tab_all[2 * i], tab_all[2 * i + 1]) for i in range(8)], axis=1)
    s16 = jnp.concatenate([s8, jnp.full((8, 1024), -1.0, jnp.float32)], axis=0)
    kept = s16 >= 0.0
    bm = ones_where((iota((1024, 128), 0) >> 6) == iota((1024, 128), 1))
    bt = ones_where((iota((128, 1024), 1) >> 6) == iota((128, 1024), 0))
    n_ps = fdot(jnp.where(kept, 1.0, 0.0), bm)
    offs = fdot(n_ps, ones_where(l0 < l1))
    off_l = fdot(jnp.minimum(offs, 255.0), bt)
    cold = kept & (hot16 < 0.5)
    rk[...] = jnp.where(cold, off_l + s16, -1.0)
    kc[...] = jnp.where(cold, 1.0, 0.0)
    sh[...] = jnp.broadcast_to(jnp.max(jnp.where(hot16 > 0.5, s16, -1.0), **DOWN), (8, 1024))
    ring(1)
    for p in range(GRP):
        at_p = block_at(p, CAP_C)
        disp[at_p, :] = ones_where(iota((CAP_C, 1024), 0).astype(jnp.float32) == rk[p : p + 1, :])
        kexp[at_p, :] = jnp.broadcast_to(kc[p : p + 1, :], (CAP_C, 1024)).astype(jnp.bfloat16)
        ring(1)
    n_e = lax.dot_general(bt, kexp[...], (((1,), (1,)), ((), ())), preferred_element_type=F32)
    most = jnp.max(jnp.sum(n_e, **DOWN), **ACROSS)
    row_most = jnp.max(jnp.sum(n_e, **ACROSS), **DOWN)
    fits = jnp.where((most <= CAP_C) & (row_most <= 32.0 * CAP_B), 1.0, 0.0)
    ok_t[0] = jnp.broadcast_to(fits, TILE)
    wide = (256, 256)
    os_e = fdot(ones_where(l1 < l0), n_e)
    oc_e = fdot(n_e, ones_where(((iota(wide, 0) >> 5) < (iota(wide, 1) >> 5)) & ((iota(wide, 0) & 31) == 0)))
    e_row = ones_where((iota((256, 128), 0) >> 4) == iota((256, 128), 1))
    n_f = fdot(e_row, n_e)
    q_k = (iota(wide, 1) & 31).astype(jnp.float32) - fdot(e_row, jnp.minimum(os_e, 255.0))
    q_r = (iota(wide, 0) & 15).astype(jnp.float32) - fdot(e_row, jnp.minimum(oc_e, 255.0))
    pack[...] = ones_where((q_k == q_r) & (q_k >= 0.0) & (q_k < n_f))
    ring(RING_AG - at[0])

    drain(toks.at[first(768)], p2_r)

    def disp_task(c):
        cols = block_at(c, 256)
        block = jnp.dot(disp[...], toks[:, cols], preferred_element_type=F32).astype(jnp.bfloat16)
        rows_c[:, :, cols] = block.reshape(GRP, CAP_C, 256)

    ring(8, disp_task)
    arr[pos] = rows_c[pos]
    ok_grp[pos] = ok_t[0]

    def x_send(src, dst, s_sem, r_sem):
        def task(i):
            part = block_at(i, 8)
            for k in (1, 7, 2, 3, 4, 5, 6):
                remote(src.at[(pos + k) % GRP, part], dst.at[pos, part], s_sem, r_sem, xdev(k)).start()
        return task

    for k in range(1, GRP):
        remote(ok_t.at[0], ok_grp.at[pos], ok_s, ok_r, xdev(k)).start()
    ring(4, x_send(rows_c, arr, xd_s, xd_r))

    def hot_task(i):
        lanes = block_at(i, 128)
        slots = sh[0:1, lanes]
        r_i = iota((64, 128), 0)
        mine_rows = (r_i >> 5) == (iota((64, 128), 1) >> 6)
        pick = ones_where(mine_rows & ((r_i & 31).astype(jnp.float32) == slots))
        out = jnp.dot(pick, toks[block_at(i, 128), :], preferred_element_type=F32)
        rows_h[block_at(i, 64), :] = out.astype(jnp.bfloat16)

    ring(8, hot_task)
    ring(RING_X1)
    drain(others(arr), xd_r)
    drain(others(ok_grp), ok_r)
    ok_t[1] = jnp.min(ok_grp[...], axis=0)
    for cp in full:
        cp.wait()

    def up_task(c):
        cols = block_at(c, 256)
        x = arr[...].reshape(GRP * CAP_C, MODEL)
        a = jnp.dot(x, cg[:, cols], preferred_element_type=F32)
        b = jnp.dot(x, cu[:, cols], preferred_element_type=F32)
        hid[:, cols] = (jax.nn.silu(a) * b).astype(jnp.bfloat16)

    def down_task(c):
        cols = block_at(c, 512)
        y = jnp.dot(hid[...], cd[:, cols], preferred_element_type=F32).astype(jnp.bfloat16)
        y_c[:, :, cols] = y.reshape(GRP, CAP_C, 512)

    ring(3, up_task)
    ring(4, down_task)
    home_c[pos] = y_c[pos]
    ring(4, x_send(y_c, home_c, xb_s, xb_r))
    ring(RING_X2)
    drain(others(home_c), xb_r)

    def pack_task(c):
        cols = block_at(c, 512)
        block = jnp.dot(pack[...], home_c[:, :, cols].reshape(GRP * CAP_C, 512), preferred_element_type=F32)
        ret_c[:, :, cols] = block.astype(jnp.bfloat16).reshape(PLN, CAP_B, 512)

    ring(4, pack_task)
    cold_home[grp] = ret_c[grp]
    ok_all[grp] = ok_t[1]
    ring(1)
    for k in FAR:
        peer = plane_peer(grp, k)
        remote(ret_c.at[peer], cold_home.at[grp], pr_s, pr_r, peer * GRP + pos).start()
    for k in range(1, PLN):
        remote(ok_t.at[1], ok_all.at[grp], oa_s, oa_r, pdev(k)).start()
    ring(T)

    drain(others(cnt_all), cnt_s)
    drain(others(tab_all), tab_s)
    drain(others(hot_all), hot_s)
    drain(toks.at[first(96)], a1_s)
    drain(toks.at[first(96)], b1_s)
    drain(toks.at[first(768)], p2_s)
    drain(others(ok_grp), ok_s)
    drain(others(arr), xd_s)
    drain(others(home_c), xb_s)
    drain(inj, inj_s)
    drain(recv, ring_s)
    drain(st, st_sem)
    drain(xr, par_s)
    drain(xr, par_r)
    drain(others(ok_all), oa_s)
    drain(others(ok_all), oa_r)
    drain(others(cold_home), pr_s)
    drain(others(cold_home), pr_r)


def main_call(tokens, ids_t, gat_t, cnt_t, w_gate, w_up, w_down):
    dma = pltpu.SemaphoreType.DMA
    bf, f32 = jnp.bfloat16, jnp.float32
    vm, an = pl.BlockSpec(memory_space=VMEM), pl.BlockSpec(memory_space=ANY)
    chunks = lambda n: VMEM((n, CH_R, CH_C), bf)
    tile = lambda *n: VMEM((*n, *TILE), f32)
    rows = VMEM((GRP, CAP_C, MODEL), bf)
    out = jax.ShapeDtypeStruct
    return pl.pallas_call(
        main_kernel,
        out_shape=(
            out((512, MODEL), bf), out((T, CH_R, CH_C), bf), out((T, CH_R, CH_C), bf), out((PLN, CAP_B, MODEL), bf),
            out((128, 512), f32), out((128, 256), f32), out((PLN, *TILE), f32), out(TILE, jnp.int32),
        ),
        in_specs=[vm, vm, vm, vm, an, an, an],
        out_specs=(vm, an, an, vm, vm, vm, vm, vm),
        scratch_shapes=[
            chunks(K), chunks(K), chunks(K), chunks(N_RING),
            VMEM((MODEL, FFN), bf), VMEM((MODEL, FFN), bf), VMEM((FFN, MODEL), bf),
            VMEM((1024, MODEL), bf), rows, rows, rows, rows, VMEM((PLN, CAP_B, MODEL), bf), VMEM((GRP * CAP_C, FFN), bf),
            tile(PLN), tile(PLN), tile(PLN), VMEM((GRP, *TILE), jnp.int32), tile(PLN), tile(2), tile(), tile(2), tile(GRP),
            VMEM((16, 1024), f32), VMEM((16, 1024), f32), VMEM((8, 1024), f32), VMEM((256, 1024), bf), VMEM((256, 1024), bf),
            VMEM((256, 256), bf), VMEM((512, 128), f32), VMEM((256, 128), f32),
            dma((32,)), dma((K // INJ,)), dma((N_SEM,)),
        ],
        compiler_params=pltpu.CompilerParams(collective_id=0, **EFFECTS, vmem_limit_bytes=60 * MIB),
    )(tokens, ids_t, gat_t, cnt_t, w_gate, w_up, w_down)


def hot_kernel(info, st, xr, wg, wu, wd, x, y, hg, hu, hd, sems):
    core = lax.axis_index("ep") % 2
    first, second = info[0, 0], info[1, 0]
    for k in range(K):
        sem = sems.at[k // 24]
        pltpu.make_async_copy(st.at[first + k], chunk_of(hg, hu, hd, core, k), sem).start()
        pltpu.make_async_copy(xr.at[second + k], chunk_of(hg, hu, hd, 1 - core, k), sem).start()
    for i, (s, d) in enumerate(((wg.at[0], hg), (wu.at[0], hu), (wd.at[0], hd))):
        pltpu.make_async_copy(s, d, sems.at[i]).wait()
    ffn_rows(x, y, hg, hu, hd)


def hot_call(info, st, xr, w_gate, w_up, w_down, x):
    bf = jnp.bfloat16
    vm, an = pl.BlockSpec(memory_space=VMEM), pl.BlockSpec(memory_space=ANY)
    return pl.pallas_call(
        hot_kernel,
        out_shape=jax.ShapeDtypeStruct(x.shape, bf),
        in_specs=[pl.BlockSpec(memory_space=pltpu.SMEM), an, an, an, an, an, vm],
        out_specs=vm,
        scratch_shapes=[VMEM((MODEL, FFN), bf), VMEM((MODEL, FFN), bf), VMEM((FFN, MODEL), bf), pltpu.SemaphoreType.DMA((3,))],
        compiler_params=pltpu.CompilerParams(vmem_limit_bytes=40 * MIB),
    )(info, st, xr, w_gate, w_up, w_down, x)


def final_kernel(y, tok, gh, gc, cold, out, home, acc, row_s, row_r):
    me = lax.axis_index("ep")
    grp, pos = me // GRP, me % GRP
    bar = pltpu.get_barrier_semaphore()
    for k in range(1, PLN):
        pl.semaphore_signal(bar, inc=1, device_id={"ep": ((grp + k) % PLN) * GRP + pos}, device_id_type=MESH)
    pl.semaphore_wait(bar, PLN - 1)
    for k in FAR:
        peer = plane_peer(grp, k)
        remote(y.at[peer], home.at[grp], row_s, row_r, peer * GRP + pos).start()
    home[grp] = y[grp]

    def pieces(g):
        g1 = g.astype(jnp.bfloat16)
        r1 = g - g1.astype(jnp.float32)
        g2 = r1.astype(jnp.bfloat16)
        g3 = (r1 - g2.astype(jnp.float32)).astype(jnp.bfloat16)
        return jnp.concatenate([g1, g2, g3], axis=0)

    def add(g, vals):
        parts = jnp.dot(g, vals, preferred_element_type=F32)
        return parts[:64] + (parts[64:128] + parts[128:])

    w_c, w_h = pieces(gc[0:64, :]), pieces(gh[0:64, :])
    for c in range(4):
        cols = block_at(c, 512)
        vals = cold[:, :, cols].reshape(PLN * CAP_B, 512)
        acc[:, cols] = tok[:, cols].astype(jnp.float32) + add(w_c, vals)
    drain(others(home), row_r)
    for c in range(4):
        cols = block_at(c, 512)
        vals = home[:, :, cols].reshape(512, 512)
        out[:, cols] = (acc[:, cols] + add(w_h, vals)).astype(jnp.bfloat16)
    drain(others(home), row_s)


def final_call(y, tokens, gh, gc, cold):
    bf = jnp.bfloat16
    vm = pl.BlockSpec(memory_space=VMEM)
    return pl.pallas_call(
        final_kernel,
        out_shape=jax.ShapeDtypeStruct((64, MODEL), bf),
        in_specs=[vm] * 5,
        out_specs=vm,
        scratch_shapes=[VMEM((PLN, 32, MODEL), bf), VMEM((64, MODEL), jnp.float32), pltpu.SemaphoreType.DMA, pltpu.SemaphoreType.DMA],
        compiler_params=pltpu.CompilerParams(collective_id=1, **EFFECTS, vmem_limit_bytes=40 * MIB),
    )(y, tokens, gh, gc, cold)


def sparse_step(tokens, expert_ids, gate_w, route_counts, w_gate, w_up, w_down):
    ids_t = jnp.concatenate([expert_ids.T, expert_ids.T], axis=1)
    gat_t = jnp.concatenate([gate_w.T, gate_w.T], axis=1)
    cnt_t = jnp.broadcast_to(route_counts, TILE)
    rows_h, st, xr, cold, gh, gc, ok_all, info = main_call(tokens, ids_t, gat_t, cnt_t, w_gate, w_up, w_down)
    y_h = hot_call(info, st, xr, w_gate, w_up, w_down, rows_h)
    out = final_call(y_h.reshape(PLN, 32, MODEL), tokens, gh, gc, cold)
    return out, jnp.min(ok_all) > 0.5


def solution(mesh):
    group_size = mesh.shape["ep"]
    row_spec = P(("dp", "ep"))

    def local_step(*args):
        fast, ok = sparse_step(*args)
        return lax.cond(ok, lambda: fast, lambda: dense_step(group_size, *args))

    return jax.shard_map(
        local_step,
        mesh=mesh,
        in_specs=(row_spec, row_spec, row_spec, row_spec, P("ep"), P("ep"), P("ep")),
        out_specs=row_spec,
        check_vma=False,
    )
```

time: 859 us -> 177 us (0.21)
  the two profiles are of different devices: /device:TPU:2 before, /device:TPU:1 now
where the time goes in v2:
time: 177 us; the launch traced here: 176 us
  Pallas kernels  164 us (93%)
  local copies, waits for them, and re-layouts  7.95 us (4%)
  other arithmetic  3.47 us (2%)
    pallas_call x1, Pallas kernels, main_call(): pl.pallas_call(main_kernel, out_shape=(out((512, MODEL), bf), out((T, CH_...  122 us
    pallas_call x1, Pallas kernels, final_call(): pl.pallas_call(final_kernel, out_shape=jax.ShapeDtypeStruct((64, MODEL),...  33.5 us
    pallas_call x1, Pallas kernels, hot_call(): pl.pallas_call(hot_kernel, out_shape=jax.ShapeDtypeStruct(x.shape, bf), i...  8.59 us
    unnamed x25, local copies, waits for them, and re-layouts  6.71 us

profile of v2, /device:TPU:1, one launch (start us, length us, event | category | flops | bytes accessed | tf_op | source)
XLA Modules:
  0.0 176.5 jit_solution(6549272124838182808)
XLA Ops:
  0.0 1.2 broadcast_in_dim.31.cnt
  1.2 1.4 pad_add_fusion.ids
  2.7 1.4 pad_maximum_fusion.gat
  4.1 121.9 %shard_map.75 = (bf16[512,2048]{1,0:T(8,128)(2,1)}, bf16[93,128,256]{2,1,0:T(8,128)(2,1)}, bf16[93,128,256]{2,1,0:T(8,128)(2,1)}, bf16[16,16,2048]{2,1,0:T(8,128...) custom-call(bf16[64,2048]{1,0:T(8,128)(2,1)} %tok.3, ...), custom_call_target="tpu_custom_call" | custom-call | tf_op jit(solution)/shard_map/pallas_call | solution.py:466
  126.0 0.0 copy-start
  126.0 2.7 %copy-done = bf16[93,128,256]{2,1,0:T(8,128)(2,1)S(1)} copy-done((bf16[93,128,256]{2,1,0:T(8,128)(2,1)S(1)}, bf16[93,128,256]{2,1,0:T(8,128)(2,1)}, u32[]{:S(2)}) %copy-start) | copy-done | bytes 6094872
  128.8 0.0 copy-start.1
  128.8 1.6 copy-done.1
  130.4 0.0 copy-start.5
  130.4 0.7 copy-done.5
  131.0 0.0 copy-start.2
  131.0 0.0 copy-start.3
  131.0 0.0 copy-start.4
  131.0 0.0 copy-start.12
  131.1 0.0 copy-start.7
  131.1 0.0 copy-start.14
  131.1 0.0 copy-start.15
  131.1 0.0 copy-start.16
  131.1 8.6 %shard_map.76 = bf16[512,2048]{1,0:T(8,128)(2,1)S(1)} custom-call(s32[8,128]{1,0:T(8,128)S(1)} %copy-done.5, bf16[93,128,256]{2,1,0:T(8,128)(2,1)S(1)} %copy-done, bf16[93,128,256]{2,1,0:T(8,128)(2,1)} %get-tuple-element.41.xr, bf16[1,2048,768]{2,1,0:T(8,128)(2,1)} %wg.3, bf16[1,2048,768]{2,1,0:T(8,128)(2,1)} %wu.3, bf16[1,768,2048]{2,1,0:T(8,128)(2,1)} %wd.3, ...), custom_call_target="tpu_custom_call" | custom-call | tf_op jit(solution)/shard_map/pallas_call | solution.py:502
  139.7 0.0 copy-done.2
  139.7 0.0 copy-done.3
  139.7 0.0 copy-done.4
  139.7 0.0 copy-done.8
  139.7 33.5 %shard_map.77 = bf16[64,2048]{1,0:T(8,128)(2,1)} custom-call(bf16[16,32,2048]{2,1,0:T(8,128)(2,1)S(1)} %bitcast.49, bf16[64,2048]{1,0:T(8,128)(2,1)S(1)} %copy-done.8, f32[128,512]{1,0:T(8,128)S(1)} %copy-done.3, f32[128,256]{1,0:T(8,128)S(1)} %copy-done.4, bf16[16,16,2048]{2,1,0:T(8,128)(2,1)S(1)} %copy-done.2), custom_call_target="tpu_custom_call" | custom-call | tf_op jit(solution)/shard_map/pallas_call | solution.py:551
  173.3 0.0 copy-done.12
  173.3 0.6 reduce_min.9
  174.5 0.0 copy-done.7
  174.6 0.0 copy-done.14
  174.6 0.0 copy-done.15
  174.6 0.0 copy-done.16
  174.6 0.2 conditional.1
  174.8 1.7 copy.43
  (1 shorter events, 0.0 us)
Async XLA Ops:
  126.0 2.7 %copy-start = (bf16[93,128,256]{2,1,0:T(8,128)(2,1)S(1)}, bf16[93,128,256]{2,1,0:T(8,128)(2,1)}, u32[]{:S(2)}) copy-start(bf16[93,128,256]{2,1,0:T(8,128)(2,1)} %get-tuple-element.40.st) | copy-start | bytes 18284548
  128.8 1.6 copy-start.1
  130.4 0.7 copy-start.5
  131.0 8.7 %copy-start.2 = (bf16[16,16,2048]{2,1,0:T(8,128)(2,1)S(1)}, bf16[16,16,2048]{2,1,0:T(8,128)(2,1)}, u32[]{:S(2)}) copy-start(bf16[16,16,2048]{2,1,0:T(8,128)(2,1)} %get-tuple-element.45.cold) | copy-start | bytes 3145732
  131.0 8.7 %copy-start.3 = (f32[128,512]{1,0:T(8,128)S(1)}, f32[128,512]{1,0:T(8,128)}, u32[]{:S(2)}) copy-start(f32[128,512]{1,0:T(8,128)} %get-tuple-element.43.gh) | copy-start | bytes 786436
  131.0 8.7 %copy-start.4 = (f32[128,256]{1,0:T(8,128)S(1)}, f32[128,256]{1,0:T(8,128)}, u32[]{:S(2)}) copy-start(f32[128,256]{1,0:T(8,128)} %get-tuple-element.44.gc) | copy-start | bytes 393220
  131.0 8.7 %copy-start.8 = (bf16[64,2048]{1,0:T(8,128)(2,1)S(1)}, bf16[64,2048]{1,0:T(8,128)(2,1)}, u32[]{:S(2)}) copy-start(bf16[64,2048]{1,0:T(8,128)(2,1)} %tok.3) | copy-start | bytes 786436
  131.0 42.2 %copy-start.12 = (f32[16,8,128]{2,1,0:T(8,128)S(1)}, f32[16,8,128]{2,1,0:T(8,128)}, u32[]{:S(2)}) copy-start(f32[16,8,128]{2,1,0:T(8,128)} %get-tuple-element.38) | copy-start | bytes 196612
  131.1 43.5 %copy-start.7 = (bf16[1,2048,768]{2,1,0:T(8,128)(2,1)S(1)}, bf16[1,2048,768]{2,1,0:T(8,128)(2,1)}, u32[]{:S(2)}) copy-start(bf16[1,2048,768]{2,1,0:T(8,128)(2,1)} %wg.3) | copy-start | bytes 9437188
  131.1 43.5 %copy-start.14 = (s32[64,8]{0,1:T(8,128)S(1)}, s32[64,8]{0,1:T(8,128)}, u32[]{:S(2)}) copy-start(s32[64,8]{0,1:T(8,128)} %param.10) | copy-start | bytes 6148
  131.1 43.5 %copy-start.15 = (f32[64,8]{0,1:T(8,128)S(1)}, f32[64,8]{0,1:T(8,128)}, u32[]{:S(2)}) copy-start(f32[64,8]{0,1:T(8,128)} %param.11) | copy-start | bytes 6148
  131.1 43.5 %copy-start.16 = (s32[1,128]{1,0:T(1,128)S(1)}, s32[1,128]{1,0:T(1,128)}, u32[]{:S(2)}) copy-start(s32[1,128]{1,0:T(1,128)} %param.12) | copy-start | bytes 1540

commit v3 on v2

--- a/solution.py
+++ b/solution.py
@@ -24,7 +24,8 @@
 N_RING = K + 2 * D
 N_SEM = 32
 INJ = 12
-CAP_B = 16
+PITCH = 32
+CAP_B = 24
 RING_AG = 44
 RING_X1, RING_X2 = 8, 12
 FAR = (10, 6, 14, 9, 11, 2, 8, 5, 7, 13, 15, 1, 3, 4, 12)
@@ -49,22 +50,31 @@
 
 
 def dense_step(group_size, tokens, expert_ids, gate_w, route_counts, w_gate, w_up, w_down):
-    tok_n = expert_ids.shape[0]
-    n_local = w_gate.shape[0]
-    model_dim = w_gate.shape[1]
-    n_exp = n_local * group_size
-    cap_rows = tok_n // 2
+    bf = jnp.bfloat16
+    tok_n, top_n = expert_ids.shape
+    n_exp = w_gate.shape[0] * group_size
+    cap_rows, step = tok_n // 2, 4
     buf_pos = place_rows(expert_ids, route_counts[0], cap_rows, n_exp)
-    disp_mat = jnp.any(jnp.arange(n_exp * cap_rows)[:, None, None] == buf_pos[None, :, :], axis=2).astype(jnp.bfloat16)
-    packed = jnp.dot(disp_mat, tokens, preferred_element_type=F32).astype(jnp.bfloat16)
-    packed = packed.reshape(group_size, n_local, cap_rows, model_dim)
-    arrived = lax.all_to_all(packed, "ep", 0, 2, tiled=True)
-    expert_out = expert_ffn(arrived.reshape(n_local, group_size * cap_rows, model_dim), w_gate, w_up, w_down)
-    returned = lax.all_to_all(expert_out.reshape(1, n_local, group_size * cap_rows, model_dim), "ep", 2, 0, tiled=True)
-    picked = jnp.take(returned.reshape(n_exp * cap_rows, model_dim), jnp.maximum(buf_pos, 0), axis=0)
-    weights = jnp.where(buf_pos >= 0, gate_w, 0.0)
-    total_f32 = tokens.astype(jnp.float32) + jnp.sum(weights[:, :, None] * picked.astype(jnp.float32), axis=1)
-    return total_f32.astype(jnp.bfloat16)
+    rows = jnp.arange(n_exp * step)
+
+    def exchange(x):
+        return lax.all_to_all(x.reshape(group_size, step, -1), "ep", 0, 0, tiled=True)
+
+    def batch(i, total):
+        slot = jnp.where(buf_pos >= 0, buf_pos % cap_rows - i * step, -1)
+        row = jnp.where((slot >= 0) & (slot < step), expert_ids * step + slot, -1)
+        put = jnp.zeros((n_exp * step, tok_n), bf)
+        for j in range(top_n):
+            put = put + (rows[:, None] == row[None, :, j]).astype(bf)
+        packed = jnp.dot(put, tokens, preferred_element_type=F32).astype(bf)
+        y = expert_ffn(exchange(packed).reshape(1, n_exp * step, MODEL), w_gate, w_up, w_down)
+        back = exchange(y).reshape(n_exp * step, MODEL)
+        for j in range(top_n):
+            got = (rows[None, :] == row[:, j][:, None]).astype(bf)
+            total = total + gate_w[:, j][:, None] * jnp.dot(got, back, preferred_element_type=F32)
+        return total
+
+    return lax.fori_loop(0, cap_rows // step, batch, tokens.astype(F32)).astype(bf)
 
 
 def chunk_of(wg, wu, wd, half, k):
@@ -311,15 +321,15 @@
         ght[block_at(g, 32), :] = jnp.where(iota((32, 128), 0).astype(jnp.float32) == s_h, w_h, 0.0)
         n = jnp.sum(jnp.where((s >= 0.0) & (lane < 64), 1.0 - h, 0.0), **ACROSS)
         off = jnp.zeros((1, 1), jnp.float32)
-        acc = jnp.zeros((16, 128), jnp.float32)
-        r_i = iota((16, 128), 0).astype(jnp.float32)
+        acc = jnp.zeros((PITCH, 128), F32)
+        r_i = iota((PITCH, 128), 0).astype(F32)
         for p in range(GRP):
             s_p = s[p : p + 1, :]
-            use = (s_p >= 0.0) & (h[p : p + 1, :] < 0.5)
+            use = (s_p >= 0.0) & (h[p : p + 1, :] < 0.5) & (s_p + off < CAP_B)
             r_p = jnp.where(use, s_p + off, -1.0)
             acc = acc + jnp.where(r_i == r_p, w[p : p + 1, :], 0.0)
             off = off + n[p : p + 1, :]
-        gct[block_at(g, 16), :] = acc
+        gct[block_at(g, PITCH), :] = acc
 
     ring(16, gate_task)
     gh[...] = ght[...].T
@@ -351,13 +361,13 @@
     row_most = jnp.max(jnp.sum(n_e, **ACROSS), **DOWN)
     fits = jnp.where((most <= CAP_C) & (row_most <= 32.0 * CAP_B), 1.0, 0.0)
     ok_t[0] = jnp.broadcast_to(fits, TILE)
-    wide = (256, 256)
+    wide, tall = (256, 256), (512, 256)
     os_e = fdot(ones_where(l1 < l0), n_e)
     oc_e = fdot(n_e, ones_where(((iota(wide, 0) >> 5) < (iota(wide, 1) >> 5)) & ((iota(wide, 0) & 31) == 0)))
-    e_row = ones_where((iota((256, 128), 0) >> 4) == iota((256, 128), 1))
+    e_row = ones_where((iota((512, 128), 0) >> 5) == iota((512, 128), 1))
     n_f = fdot(e_row, n_e)
-    q_k = (iota(wide, 1) & 31).astype(jnp.float32) - fdot(e_row, jnp.minimum(os_e, 255.0))
-    q_r = (iota(wide, 0) & 15).astype(jnp.float32) - fdot(e_row, jnp.minimum(oc_e, 255.0))
+    q_k = (iota(tall, 1) & 31).astype(jnp.float32) - fdot(e_row, jnp.minimum(os_e, 255.0))
+    q_r = (iota(tall, 0) & 31).astype(jnp.float32) - fdot(e_row, jnp.minimum(oc_e, 255.0))
     pack[...] = ones_where((q_k == q_r) & (q_k >= 0.0) & (q_k < n_f))
     ring(RING_AG - at[0])
 
@@ -422,15 +432,18 @@
     def pack_task(c):
         cols = block_at(c, 512)
         block = jnp.dot(pack[...], home_c[:, :, cols].reshape(GRP * CAP_C, 512), preferred_element_type=F32)
-        ret_c[:, :, cols] = block.astype(jnp.bfloat16).reshape(PLN, CAP_B, 512)
+        ret_c[:, :, cols] = block.astype(jnp.bfloat16).reshape(PLN, PITCH, 512)
 
     ring(4, pack_task)
-    cold_home[grp] = ret_c[grp]
+    few = first(CAP_B)
+    rest = pl.ds(CAP_B, PITCH - CAP_B)
+    cold_home[:, rest, :] = jnp.zeros((PLN, PITCH - CAP_B, MODEL), jnp.bfloat16)
+    cold_home[grp, few, :] = ret_c[grp, few, :]
     ok_all[grp] = ok_t[1]
     ring(1)
     for k in FAR:
         peer = plane_peer(grp, k)
-        remote(ret_c.at[peer], cold_home.at[grp], pr_s, pr_r, peer * GRP + pos).start()
+        remote(ret_c.at[peer, few], cold_home.at[grp, few], pr_s, pr_r, peer * GRP + pos).start()
     for k in range(1, PLN):
         remote(ok_t.at[1], ok_all.at[grp], oa_s, oa_r, pdev(k)).start()
     ring(T)
@@ -451,8 +464,8 @@
     drain(xr, par_r)
     drain(others(ok_all), oa_s)
     drain(others(ok_all), oa_r)
-    drain(others(cold_home), pr_s)
-    drain(others(cold_home), pr_r)
+    drain(cold_home.at[first(PLN - 1), few], pr_s)
+    drain(cold_home.at[first(PLN - 1), few], pr_r)
 
 
 def main_call(tokens, ids_t, gat_t, cnt_t, w_gate, w_up, w_down):
@@ -466,18 +479,18 @@
     return pl.pallas_call(
         main_kernel,
         out_shape=(
-            out((512, MODEL), bf), out((T, CH_R, CH_C), bf), out((T, CH_R, CH_C), bf), out((PLN, CAP_B, MODEL), bf),
-            out((128, 512), f32), out((128, 256), f32), out((PLN, *TILE), f32), out(TILE, jnp.int32),
+            out((512, MODEL), bf), out((T, CH_R, CH_C), bf), out((T, CH_R, CH_C), bf), out((PLN, PITCH, MODEL), bf),
+            out((128, 512), f32), out((128, 512), f32), out((PLN, *TILE), f32), out(TILE, jnp.int32),
         ),
         in_specs=[vm, vm, vm, vm, an, an, an],
         out_specs=(vm, an, an, vm, vm, vm, vm, vm),
         scratch_shapes=[
             chunks(K), chunks(K), chunks(K), chunks(N_RING),
             VMEM((MODEL, FFN), bf), VMEM((MODEL, FFN), bf), VMEM((FFN, MODEL), bf),
-            VMEM((1024, MODEL), bf), rows, rows, rows, rows, VMEM((PLN, CAP_B, MODEL), bf), VMEM((GRP * CAP_C, FFN), bf),
+            VMEM((1024, MODEL), bf), rows, rows, rows, rows, VMEM((PLN, PITCH, MODEL), bf), VMEM((GRP * CAP_C, FFN), bf),
             tile(PLN), tile(PLN), tile(PLN), VMEM((GRP, *TILE), jnp.int32), tile(PLN), tile(2), tile(), tile(2), tile(GRP),
             VMEM((16, 1024), f32), VMEM((16, 1024), f32), VMEM((8, 1024), f32), VMEM((256, 1024), bf), VMEM((256, 1024), bf),
-            VMEM((256, 256), bf), VMEM((512, 128), f32), VMEM((256, 128), f32),
+            VMEM((512, 256), bf), VMEM((512, 128), f32), VMEM((512, 128), f32),
             dma((32,)), dma((K // INJ,)), dma((N_SEM,)),
         ],
         compiler_params=pltpu.CompilerParams(collective_id=0, **EFFECTS, vmem_limit_bytes=60 * MIB),
@@ -535,7 +548,7 @@
     w_c, w_h = pieces(gc[0:64, :]), pieces(gh[0:64, :])
     for c in range(4):
         cols = block_at(c, 512)
-        vals = cold[:, :, cols].reshape(PLN * CAP_B, 512)
+        vals = cold[:, :, cols].reshape(512, 512)
         acc[:, cols] = tok[:, cols].astype(jnp.float32) + add(w_c, vals)
     drain(others(home), row_r)
     for c in range(4):

time: 177 us -> 187 us (1.056)
  Pallas kernels: 164 us -> 174 us
    pallas_call x1, Pallas kernels: 122 us -> 129 us  [main_call(): pl.pallas_call(main_kernel, out_shape=(out((512, MODEL), bf), out((T, CH_...]
    pallas_call x1, Pallas kernels: 33.5 us -> 36.7 us  [final_call(): pl.pallas_call(final_kernel, out_shape=jax.ShapeDtypeStruct((64, MODEL),...]
    unnamed x25 -> x23, local copies, waits for them, and re-layouts: 6.71 us -> 6.69 us
where the time goes in v3:
time: 187 us
  Pallas kernels  174 us (93%)
  local copies, waits for them, and re-layouts  7.93 us (4%)
  other arithmetic  4.32 us (2%)
    pallas_call x1, Pallas kernels, main_call(): pl.pallas_call(main_kernel, out_shape=(out((512, MODEL), bf), out((T, CH_...  129 us
    pallas_call x1, Pallas kernels, final_call(): pl.pallas_call(final_kernel, out_shape=jax.ShapeDtypeStruct((64, MODEL),...  36.7 us
    pallas_call x1, Pallas kernels, hot_call(): pl.pallas_call(hot_kernel, out_shape=jax.ShapeDtypeStruct(x.shape, bf), i...  8.52 us
    unnamed x23, local copies, waits for them, and re-layouts  6.69 us

profile of v3, /device:TPU:1, one launch (start us, length us, event | category | flops | bytes accessed | tf_op | source)
XLA Modules:
  0.0 187.0 jit_solution(12148946899632419139)
XLA Ops:
  0.0 1.2 broadcast_in_dim.46.cnt
  1.2 1.4 pad_maximum_fusion.gat
  2.7 1.4 pad_add_fusion.ids
  4.1 0.0 copy-start.7
  4.1 128.6 %shard_map.75 = (bf16[512,2048]{1,0:T(8,128)(2,1)}, bf16[93,128,256]{2,1,0:T(8,128)(2,1)}, bf16[93,128,256]{2,1,0:T(8,128)(2,1)}, bf16[16,32,2048]{2,1,0:T(8,128...) custom-call(bf16[64,2048]{1,0:T(8,128)(2,1)} %tok.3, ...), custom_call_target="tpu_custom_call" | custom-call | tf_op jit(solution)/shard_map/pallas_call | solution.py:479
  132.7 1.5 reduce_min.9
  134.8 0.0 copy-done.7
  134.8 0.0 copy-start
  134.8 2.7 %copy-done = bf16[93,128,256]{2,1,0:T(8,128)(2,1)S(1)} copy-done((bf16[93,128,256]{2,1,0:T(8,128)(2,1)S(1)}, bf16[93,128,256]{2,1,0:T(8,128)(2,1)}, u32[]{:S(2)}) %copy-start) | copy-done | bytes 6094872
  137.5 0.0 copy-start.2
  137.6 1.6 copy-done.2
  139.1 0.0 copy-start.5
  139.1 0.7 copy-done.5
  139.8 0.0 copy-start.1
  139.8 0.0 copy-start.3
  139.8 0.0 copy-start.4
  139.8 0.0 copy-start.6
  139.8 0.0 copy-start.10
  139.8 0.0 copy-start.11
  139.8 0.0 copy-start.12
  139.9 8.5 %shard_map.76 = bf16[512,2048]{1,0:T(8,128)(2,1)S(1)} custom-call(s32[8,128]{1,0:T(8,128)S(1)} %copy-done.5, bf16[93,128,256]{2,1,0:T(8,128)(2,1)S(1)} %copy-done, bf16[93,128,256]{2,1,0:T(8,128)(2,1)} %get-tuple-element.374.xr, bf16[1,2048,768]{2,1,0:T(8,128)(2,1)S(1)} %copy-done.7, bf16[1,2048,768]{2,1,0:T(8,128)(2,1)} %wu.3, bf16[1,768,2048]{2,1,0:T(8,128)(2,1)} %wd.3, ...), custom_call_target="tpu_custom_call" | custom-call | tf_op jit(solution)/shard_map/pallas_call | solution.py:515
  148.4 0.0 copy-done.1
  148.4 0.0 copy-done.3
  148.4 0.0 copy-done.4
  148.4 0.0 copy-done.6
  148.4 0.0 copy-done.10
  148.4 0.0 copy-done.11
  148.4 0.0 copy-done.12
  148.5 36.7 %shard_map.77 = bf16[64,2048]{1,0:T(8,128)(2,1)} custom-call(bf16[16,32,2048]{2,1,0:T(8,128)(2,1)S(1)} %bitcast.108, bf16[64,2048]{1,0:T(8,128)(2,1)S(1)} %copy-done.6, f32[128,512]{1,0:T(8,128)S(1)} %copy-done.3, f32[128,512]{1,0:T(8,128)S(1)} %copy-done.4, bf16[16,32,2048]{2,1,0:T(8,128)(2,1)S(1)} %copy-done.1), custom_call_target="tpu_custom_call" | custom-call | tf_op jit(solution)/shard_map/pallas_call | solution.py:564
  185.1 0.2 conditional.1
  185.4 1.7 copy.33
Async XLA Ops:
  4.1 130.7 %copy-start.7 = (bf16[1,2048,768]{2,1,0:T(8,128)(2,1)S(1)}, bf16[1,2048,768]{2,1,0:T(8,128)(2,1)}, u32[]{:S(2)}) copy-start(bf16[1,2048,768]{2,1,0:T(8,128)(2,1)} %wg.3) | copy-start | bytes 9437188
  134.8 2.7 %copy-start = (bf16[93,128,256]{2,1,0:T(8,128)(2,1)S(1)}, bf16[93,128,256]{2,1,0:T(8,128)(2,1)}, u32[]{:S(2)}) copy-start(bf16[93,128,256]{2,1,0:T(8,128)(2,1)} %get-tuple-element.373.st) | copy-start | bytes 18284548
  137.5 1.6 copy-start.2
  139.1 0.7 copy-start.5
  139.8 8.6 %copy-start.1 = (bf16[16,32,2048]{2,1,0:T(8,128)(2,1)S(1)}, bf16[16,32,2048]{2,1,0:T(8,128)(2,1)}, u32[]{:S(2)}) copy-start(bf16[16,32,2048]{2,1,0:T(8,128)(2,1)} %get-tuple-element.378.cold) | copy-start | bytes 6291460
  139.8 8.6 %copy-start.3 = (f32[128,512]{1,0:T(8,128)S(1)}, f32[128,512]{1,0:T(8,128)}, u32[]{:S(2)}) copy-start(f32[128,512]{1,0:T(8,128)} %get-tuple-element.376.gh) | copy-start | bytes 786436
  139.8 8.6 %copy-start.4 = (f32[128,512]{1,0:T(8,128)S(1)}, f32[128,512]{1,0:T(8,128)}, u32[]{:S(2)}) copy-start(f32[128,512]{1,0:T(8,128)} %get-tuple-element.377.gc) | copy-start | bytes 786436
  139.8 8.6 %copy-start.6 = (bf16[64,2048]{1,0:T(8,128)(2,1)S(1)}, bf16[64,2048]{1,0:T(8,128)(2,1)}, u32[]{:S(2)}) copy-start(bf16[64,2048]{1,0:T(8,128)(2,1)} %tok.3) | copy-start | bytes 786436
  139.8 8.6 %copy-start.10 = (s32[64,8]{0,1:T(8,128)S(1)}, s32[64,8]{0,1:T(8,128)}, u32[]{:S(2)}) copy-start(s32[64,8]{0,1:T(8,128)} %param.12) | copy-start | bytes 6148
  139.8 8.6 %copy-start.11 = (f32[64,8]{0,1:T(8,128)S(1)}, f32[64,8]{0,1:T(8,128)}, u32[]{:S(2)}) copy-start(f32[64,8]{0,1:T(8,128)} %param.13) | copy-start | bytes 6148
  139.8 8.6 %copy-start.12 = (s32[1,128]{1,0:T(1,128)S(1)}, s32[1,128]{1,0:T(1,128)}, u32[]{:S(2)}) copy-start(s32[1,128]{1,0:T(1,128)} %param.14) | copy-start | bytes 1540

commit v4 on v3

--- a/solution.py
+++ b/solution.py
@@ -25,6 +25,7 @@
 N_SEM = 32
 INJ = 12
 PITCH = 32
+SELF = 10
 CAP_B = 24
 RING_AG = 44
 RING_X1, RING_X2 = 8, 12
@@ -115,19 +116,6 @@
     pltpu.make_async_copy(ref, ref, sem).wait()
 
 
-def ffn_rows(x, y, wg, wu, wd):
-    def block(i, carry):
-        at = block_at(i, 256)
-        rows = x[at, :]
-        a = jnp.dot(rows, wg[...], preferred_element_type=F32)
-        b = jnp.dot(rows, wu[...], preferred_element_type=F32)
-        h = (jax.nn.silu(a) * b).astype(jnp.bfloat16)
-        y[at, :] = jnp.dot(h, wd[...], preferred_element_type=F32).astype(jnp.bfloat16)
-        return carry
-
-    lax.fori_loop(0, x.shape[0] // 256, block, 0)
-
-
 def iota(shape, dim):
     return lax.broadcasted_iota(jnp.int32, shape, dim)
 
@@ -140,10 +128,9 @@
     return jnp.dot(a.astype(jnp.bfloat16), b.astype(jnp.bfloat16), preferred_element_type=F32)
 
 
-def main_kernel(tok, ids, gat, cnt, wg, wu, wd,
-                rows_h, st, xr, cold_home, gh, gc, ok_all, info,
-                own, inj, stage, recv, cg, cu, cd, toks, rows_c, arr, y_c, home_c, ret_c, hid,
-                sl, gt, tab_all, cnt_all, hot_all, flags, hot_t, ok_t, ok_grp, rk, kc, sh, disp, kexp, pack, ght, gct,
+def main_kernel(tok, ids, gat, cnt, wg, wu, wd, out, ok_all,
+                inj, stage, recv, xr, cg, cu, cd, toks, rows_c, arr, y_c, home_c, ret_c, cold_home, rows_h, y_h, home_h, hid, acc_ref,
+                sl, gt, tab_all, cnt_me, cnt_all, hot_all, flags, hot_t, ok_t, ok_grp, rk, kc, disp, kexp, pack, ght, gct, gh, gc,
                 dma1, inj_r, ring_r):
     me = lax.axis_index("ep")
     grp, pos = me // GRP, me % GRP
@@ -153,8 +140,12 @@
     partner = grp * GRP + xx * 2 + other
     nbr = grp * GRP + ((xx + 1 + 2 * core) % 4) * 2 + core
     wg, wu, wd = wg.at[0], wu.at[0], wd.at[0]
-    (own_sem, w0_sem, w1_sem, w2_sem, cnt_s, cnt_r, tab_s, tab_r, hot_s, hot_r, inj_s, a1_s, a1_r, b1_s, b1_r, p2_s, p2_r,
-     xd_s, xd_r, ok_s, ok_r, xb_s, xb_r, pr_s, pr_r, oa_s, oa_r, ring_s, par_s, par_r, st_sem, loc_sem) = [dma1.at[i] for i in range(32)]
+    (hh_s, hh_r, w0_sem, w1_sem, w2_sem, cnt_s, cnt_r, tab_s, tab_r, hot_s, hot_r, inj_s, a1_s, a1_r, b1_s, b1_r, p2_s, p2_r,
+     xd_s, xd_r, ok_s, ok_r, xb_s, xb_r, pr_s, pr_r, oa_s, oa_r, ring_s, par_s, par_r, loc_sem) = [dma1.at[i] for i in range(32)]
+
+    def far_peer(i):
+        z_off, y_off = (i // 4 + 2) % 4, (i % 4 + 2) % 4
+        return ((zz + z_off) % 4) * 4 + (yy + y_off) % 4
 
     def xdev(k):
         return grp * GRP + (pos + k) % GRP
@@ -162,20 +153,23 @@
     def pdev(k):
         return ((grp + k) % PLN) * GRP + pos
 
-    for k in range(K):
-        pltpu.make_async_copy(chunk_of(wg, wu, wd, core, k), own.at[k], own_sem).start()
     mine_at = block_at(grp, 64)
     pltpu.make_async_copy(tok, toks.at[mine_at], loc_sem).start()
     full = [pltpu.make_async_copy(s, d, q) for s, d, q in ((wg, cg, w0_sem), (wu, cu, w1_sem), (wd, cd, w2_sem))]
+    for cp in full:
+        cp.start()
+    cnt_me[...] = jnp.broadcast_to(cnt[...], TILE)
 
     sq = (128, 128)
     e_i = iota(sq, 0)
     named = jnp.zeros(sq, F32)
     gates = jnp.zeros(sq, F32)
+    ids2 = jnp.concatenate([ids[...], ids[...]], axis=1)
+    gat2 = jnp.concatenate([gat[...], gat[...]], axis=1)
     for j in range(8):
-        hit_j = ids[j : j + 1, :] == e_i
+        hit_j = ids2[j : j + 1, :] == e_i
         named = jnp.where(hit_j, 1.0, named)
-        gates = jnp.where(hit_j, gat[j : j + 1, :], gates)
+        gates = jnp.where(hit_j, gat2[j : j + 1, :], gates)
     l0, l1 = iota(sq, 0), iota(sq, 1)
     slot = fdot(named, ones_where(((l0 >> 6) == (l1 >> 6)) & (l0 < l1)))
     sl[...] = jnp.where((named > 0.5) & (slot < 32.0), slot, -1.0).reshape(PLN, *TILE)
@@ -189,8 +183,8 @@
     pl.semaphore_wait(bar, GRP - 1 + PLN - 1)
 
     for k in range(1, GRP):
-        remote(cnt, cnt_all.at[pos], cnt_s, cnt_r, xdev(k)).start()
-    cnt_all[pos] = cnt[...]
+        remote(cnt_me, cnt_all.at[pos], cnt_s, cnt_r, xdev(k)).start()
+    cnt_all[pos] = cnt_me[...]
 
     def half_at(z, y, h):
         return pl.ds(pl.multiple_of(((z % 4) * 4 + (y % 4)) * 64 + 32 * h, 32), 32)
@@ -201,13 +195,14 @@
     for k in (1, 3, 2):
         remote(tok.at[first(32)], toks.at[half_at(zz, yy, 0)], a1_s, a1_r, plane_dev(zz, yy + k)).start()
         remote(tok.at[pl.ds(32, 32)], toks.at[half_at(zz, yy, 1)], b1_s, b1_r, plane_dev(zz + k, yy)).start()
+    for k in (1, 3, 2):
+        remote(tok.at[first(32)], toks.at[half_at(zz, yy, 0)], p2_s, p2_r, plane_dev(zz + k, yy)).start()
+        remote(tok.at[pl.ds(32, 32)], toks.at[half_at(zz, yy, 1)], p2_s, p2_r, plane_dev(zz, yy + k)).start()
     for k in range(K):
         remote(chunk_of(wg, wu, wd, other, k), inj.at[k], inj_s, inj_r.at[k // INJ], partner).start()
     for k in range(1, PLN):
         remote(sl.at[(grp + k) % PLN], tab_all.at[grp], tab_s, tab_r, pdev(k)).start()
     tab_all[grp] = sl[grp]
-    for cp in full:
-        cp.start()
 
     drain(others(cnt_all), cnt_r)
     total = jnp.sum(cnt_all[...].astype(jnp.float32), axis=0)
@@ -225,8 +220,8 @@
     hx = jnp.sum(hit * ((lane & 7) >> 1).astype(jnp.float32), **ACROSS).astype(jnp.int32)
     sign = 1 - 2 * core
     hops = (sign * (xx - hx) + 8) & 3
-    info[...] = jnp.where(iota(TILE, 0) == 0, D * hops, D * ((4 - hops) & 3))
-    drain(own, own_sem)
+    hops = jnp.max(hops.astype(F32)).astype(jnp.int32)
+    full[0].wait()
 
     def flag(i):
         row = flags[i, 0:1, :]
@@ -236,33 +231,43 @@
         if ring:
             remote(src, recv.at[t], ring_s, ring_r.at[t % N_SEM], nbr).start()
         remote(src, xr.at[t], par_s, par_r, partner).start()
-        pltpu.make_async_copy(src, st.at[t], st_sem).start()
 
     def take(t):
         pltpu.make_async_copy(recv.at[t], recv.at[t], ring_r.at[t % N_SEM]).wait()
 
-    def build(t, first):
-        a = own[t].astype(jnp.float32)
+    def own_chunk(arr_i, t):
+        if arr_i < 2:
+            k = t - 24 * arr_i
+            row, col = core * 1024 + (k // 3) * CH_R, (k % 3) * CH_C
+        else:
+            k = t - 48
+            row, col = core * 384 + (k // 8) * CH_R, (k % 8) * CH_C
+        return (cg, cu, cd)[arr_i][pl.ds(pl.multiple_of(row, CH_R), CH_R), pl.ds(pl.multiple_of(col, CH_C), CH_C)]
+
+    def build(t, first, arr_i):
+        a = own_chunk(arr_i, t).astype(jnp.float32)
         b = inj[t].astype(jnp.float32)
         if not first:
             b = jnp.where(flag(1) > 0.5, b, recv[t - D].astype(jnp.float32))
         stage[t] = jnp.where(flag(0) > 0.5, a, b).astype(jnp.bfloat16)
 
-    def head(t):
-        build(t, True)
+    def head(t, arr_i):
+        build(t, True, 0)
         send(t - 1, stage.at[t - 1])
 
-    def body(t):
+    def body(t, arr_i):
         take(t - D)
-        build(t, False)
+        build(t, False, arr_i)
         send(t - 1, stage.at[t - 1])
 
-    def tail(t):
+    def tail(t, arr_i):
         take(t - D)
+        stage[t] = recv[t - D]
         send(t, recv.at[t - D])
 
-    def last(t):
+    def last(t, arr_i):
         take(t - D)
+        stage[t] = recv[t - D]
         send(t, recv.at[t - D], ring=False)
 
     at = [0]
@@ -272,12 +277,14 @@
         end = min(base + n, T)
         while at[0] < end:
             t = at[0]
+            if t in (24, 48):
+                full[t // 24].wait()
             if t < K and t % INJ == 0:
                 drain(inj.at[pl.ds(t, INJ)], inj_r.at[t // INJ])
             if t == K:
                 send(K - 1, stage.at[K - 1])
             if t == 0:
-                build(0, True)
+                build(0, True, 0)
                 if task is not None:
                     task(0)
                 at[0] = 1
@@ -285,8 +292,8 @@
             kind, stop = (head, D) if t < D else (body, (t // INJ + 1) * INJ) if t < K else (tail, N_RING) if t < N_RING else (last, T)
             stop = min(stop, end)
 
-            def step(i, carry, kind=kind):
-                kind(i)
+            def step(i, carry, kind=kind, arr_i=t // 24):
+                kind(i, arr_i)
                 if task is not None:
                     task(i - base)
                 return carry
@@ -305,8 +312,8 @@
     pltpu.make_async_copy(tok, toks.at[mine_at], loc_sem).wait()
     drain(toks.at[first(96)], a1_r)
     drain(toks.at[first(96)], b1_r)
-    for k in (2, 1, 3):
-        for i in range(4):
+    for k in (1, 3, 2):
+        for i in range(1, 4):
             a_at, b_at = half_at(zz, yy + i, 0), half_at(zz + i, yy, 1)
             remote(toks.at[a_at], toks.at[a_at], p2_s, p2_r, plane_dev(zz + k, yy)).start()
             remote(toks.at[b_at], toks.at[b_at], p2_s, p2_r, plane_dev(zz, yy + k)).start()
@@ -349,7 +356,6 @@
     cold = kept & (hot16 < 0.5)
     rk[...] = jnp.where(cold, off_l + s16, -1.0)
     kc[...] = jnp.where(cold, 1.0, 0.0)
-    sh[...] = jnp.broadcast_to(jnp.max(jnp.where(hot16 > 0.5, s16, -1.0), **DOWN), (8, 1024))
     ring(1)
     for p in range(GRP):
         at_p = block_at(p, CAP_C)
@@ -394,22 +400,18 @@
     ring(4, x_send(rows_c, arr, xd_s, xd_r))
 
     def hot_task(i):
-        lanes = block_at(i, 128)
-        slots = sh[0:1, lanes]
-        r_i = iota((64, 128), 0)
-        mine_rows = (r_i >> 5) == (iota((64, 128), 1) >> 6)
-        pick = ones_where(mine_rows & ((r_i & 31).astype(jnp.float32) == slots))
-        out = jnp.dot(pick, toks[block_at(i, 128), :], preferred_element_type=F32)
-        rows_h[block_at(i, 64), :] = out.astype(jnp.bfloat16)
+        for half in range(2):
+            peer = far_peer(2 * i + half)
+            slots = jnp.max(jnp.where(hot_t[...] > 0.5, tab_all[peer], -1.0), **DOWN)
+            pick = ones_where(iota((32, 64), 0).astype(F32) == slots[:, 0:64])
+            out_rows = jnp.dot(pick, toks[block_at(peer, 64), :], preferred_element_type=F32)
+            rows_h[block_at(2 * i + half, 32), :] = out_rows.astype(jnp.bfloat16)
 
     ring(8, hot_task)
     ring(RING_X1)
     drain(others(arr), xd_r)
     drain(others(ok_grp), ok_r)
     ok_t[1] = jnp.min(ok_grp[...], axis=0)
-    for cp in full:
-        cp.wait()
-
     def up_task(c):
         cols = block_at(c, 256)
         x = arr[...].reshape(GRP * CAP_C, MODEL)
@@ -448,6 +450,70 @@
         remote(ok_t.at[1], ok_all.at[grp], oa_s, oa_r, pdev(k)).start()
     ring(T)
 
+    drain(xr, par_r)
+    near, cross = D * (hops & 3), D * ((4 - hops) & 3)
+
+    def gather_up(arr, base):
+        def copy(i, carry):
+            cols = pl.ds(pl.multiple_of((i % 3) * CH_C, CH_C), CH_C)
+            for src, off, half in ((stage, near, core), (xr, cross, other)):
+                rows = pl.ds(pl.multiple_of(half * 1024 + (i // 3) * CH_R, CH_R), CH_R)
+                arr[rows, cols] = src[off + base + i]
+            return carry
+
+        lax.fori_loop(0, 24, copy, 0)
+
+    def gather_down(i, carry):
+        cols = pl.ds(pl.multiple_of((i % 8) * CH_C, CH_C), CH_C)
+        for src, off, half in ((stage, near, core), (xr, cross, other)):
+            rows = pl.ds(pl.multiple_of(half * 384 + (i // 8) * CH_R, CH_R), CH_R)
+            cd[rows, cols] = src[off + 48 + i]
+        return carry
+
+    gather_up(cg, 0)
+    gather_up(cu, 24)
+    lax.fori_loop(0, 24, gather_down, 0)
+
+    for blk in range(2):
+        x = rows_h[block_at(blk, 256), :]
+        for c in range(3):
+            cols = block_at(c, 256)
+            a = jnp.dot(x, cg[:, cols], preferred_element_type=F32)
+            b = jnp.dot(x, cu[:, cols], preferred_element_type=F32)
+            hid[:, cols] = (jax.nn.silu(a) * b).astype(jnp.bfloat16)
+        for c in range(4):
+            cols = block_at(c, 512)
+            y = jnp.dot(hid[...], cd[:, cols], preferred_element_type=F32).astype(jnp.bfloat16)
+            y_h[block_at(blk, 8), :, cols] = y.reshape(8, 32, 512)
+        for i in range(8 * blk, 8 * blk + 8):
+            if i != SELF:
+                peer = far_peer(i)
+                remote(y_h.at[i], home_h.at[grp], hh_s, hh_r, peer * GRP + pos).start()
+    home_h[grp] = y_h[SELF]
+
+    def pieces(g):
+        g1 = g.astype(jnp.bfloat16)
+        r1 = g - g1.astype(F32)
+        g2 = r1.astype(jnp.bfloat16)
+        g3 = (r1 - g2.astype(F32)).astype(jnp.bfloat16)
+        return jnp.concatenate([g1, g2, g3], axis=0)
+
+    def add(g, vals):
+        parts = jnp.dot(g, vals, preferred_element_type=F32)
+        return parts[:64] + (parts[64:128] + parts[128:])
+
+    w_c, w_h = pieces(gc[0:64, :]), pieces(gh[0:64, :])
+    drain(cold_home.at[first(PLN - 1), few], pr_r)
+    for c in range(4):
+        cols = block_at(c, 512)
+        vals = cold_home[:, :, cols].reshape(512, 512)
+        acc_ref[:, cols] = tok[:, cols].astype(F32) + add(w_c, vals)
+    drain(others(home_h), hh_r)
+    for c in range(4):
+        cols = block_at(c, 512)
+        vals = home_h[:, :, cols].reshape(512, 512)
+        out[:, cols] = (acc_ref[:, cols] + add(w_h, vals)).astype(jnp.bfloat16)
+
     drain(others(cnt_all), cnt_s)
     drain(others(tab_all), tab_s)
     drain(others(hot_all), hot_s)
@@ -459,125 +525,42 @@
     drain(others(home_c), xb_s)
     drain(inj, inj_s)
     drain(recv, ring_s)
-    drain(st, st_sem)
     drain(xr, par_s)
-    drain(xr, par_r)
+    drain(others(home_h), hh_s)
     drain(others(ok_all), oa_s)
     drain(others(ok_all), oa_r)
     drain(cold_home.at[first(PLN - 1), few], pr_s)
-    drain(cold_home.at[first(PLN - 1), few], pr_r)
-
-
-def main_call(tokens, ids_t, gat_t, cnt_t, w_gate, w_up, w_down):
+
+
+def main_call(tokens, ids_t, gat_t, counts, w_gate, w_up, w_down):
     dma = pltpu.SemaphoreType.DMA
-    bf, f32 = jnp.bfloat16, jnp.float32
+    bf = jnp.bfloat16
     vm, an = pl.BlockSpec(memory_space=VMEM), pl.BlockSpec(memory_space=ANY)
     chunks = lambda n: VMEM((n, CH_R, CH_C), bf)
-    tile = lambda *n: VMEM((*n, *TILE), f32)
-    rows = VMEM((GRP, CAP_C, MODEL), bf)
-    out = jax.ShapeDtypeStruct
+    tile = lambda *n: VMEM((*n, *TILE), F32)
+    rows, back = VMEM((GRP, CAP_C, MODEL), bf), VMEM((PLN, PITCH, MODEL), bf)
+    wide, tall = VMEM((16, 1024), F32), VMEM((512, 128), F32)
     return pl.pallas_call(
         main_kernel,
-        out_shape=(
-            out((512, MODEL), bf), out((T, CH_R, CH_C), bf), out((T, CH_R, CH_C), bf), out((PLN, PITCH, MODEL), bf),
-            out((128, 512), f32), out((128, 512), f32), out((PLN, *TILE), f32), out(TILE, jnp.int32),
-        ),
+        out_shape=(jax.ShapeDtypeStruct((64, MODEL), bf), jax.ShapeDtypeStruct((PLN, *TILE), F32)),
         in_specs=[vm, vm, vm, vm, an, an, an],
-        out_specs=(vm, an, an, vm, vm, vm, vm, vm),
+        out_specs=(vm, vm),
         scratch_shapes=[
-            chunks(K), chunks(K), chunks(K), chunks(N_RING),
+            chunks(K), chunks(T), chunks(N_RING), chunks(T),
             VMEM((MODEL, FFN), bf), VMEM((MODEL, FFN), bf), VMEM((FFN, MODEL), bf),
-            VMEM((1024, MODEL), bf), rows, rows, rows, rows, VMEM((PLN, PITCH, MODEL), bf), VMEM((GRP * CAP_C, FFN), bf),
-            tile(PLN), tile(PLN), tile(PLN), VMEM((GRP, *TILE), jnp.int32), tile(PLN), tile(2), tile(), tile(2), tile(GRP),
-            VMEM((16, 1024), f32), VMEM((16, 1024), f32), VMEM((8, 1024), f32), VMEM((256, 1024), bf), VMEM((256, 1024), bf),
-            VMEM((512, 256), bf), VMEM((512, 128), f32), VMEM((512, 128), f32),
+            VMEM((1024, MODEL), bf), rows, rows, rows, rows, back, back, VMEM((512, MODEL), bf), back, back,
+            VMEM((GRP * CAP_C, FFN), bf), VMEM((64, MODEL), F32),
+            tile(PLN), tile(PLN), tile(PLN), VMEM(TILE, jnp.int32), VMEM((GRP, *TILE), jnp.int32), tile(PLN), tile(2), tile(), tile(2), tile(GRP),
+            wide, wide, VMEM((256, 1024), bf), VMEM((256, 1024), bf), VMEM((512, 256), bf), tall, tall,
+            VMEM((128, 512), F32), VMEM((128, 512), F32),
             dma((32,)), dma((K // INJ,)), dma((N_SEM,)),
         ],
-        compiler_params=pltpu.CompilerParams(collective_id=0, **EFFECTS, vmem_limit_bytes=60 * MIB),
-    )(tokens, ids_t, gat_t, cnt_t, w_gate, w_up, w_down)
-
-
-def hot_kernel(info, st, xr, wg, wu, wd, x, y, hg, hu, hd, sems):
-    core = lax.axis_index("ep") % 2
-    first, second = info[0, 0], info[1, 0]
-    for k in range(K):
-        sem = sems.at[k // 24]
-        pltpu.make_async_copy(st.at[first + k], chunk_of(hg, hu, hd, core, k), sem).start()
-        pltpu.make_async_copy(xr.at[second + k], chunk_of(hg, hu, hd, 1 - core, k), sem).start()
-    for i, (s, d) in enumerate(((wg.at[0], hg), (wu.at[0], hu), (wd.at[0], hd))):
-        pltpu.make_async_copy(s, d, sems.at[i]).wait()
-    ffn_rows(x, y, hg, hu, hd)
-
-
-def hot_call(info, st, xr, w_gate, w_up, w_down, x):
-    bf = jnp.bfloat16
-    vm, an = pl.BlockSpec(memory_space=VMEM), pl.BlockSpec(memory_space=ANY)
-    return pl.pallas_call(
-        hot_kernel,
-        out_shape=jax.ShapeDtypeStruct(x.shape, bf),
-        in_specs=[pl.BlockSpec(memory_space=pltpu.SMEM), an, an, an, an, an, vm],
-        out_specs=vm,
-        scratch_shapes=[VMEM((MODEL, FFN), bf), VMEM((MODEL, FFN), bf), VMEM((FFN, MODEL), bf), pltpu.SemaphoreType.DMA((3,))],
-        compiler_params=pltpu.CompilerParams(vmem_limit_bytes=40 * MIB),
-    )(info, st, xr, w_gate, w_up, w_down, x)
-
-
-def final_kernel(y, tok, gh, gc, cold, out, home, acc, row_s, row_r):
-    me = lax.axis_index("ep")
-    grp, pos = me // GRP, me % GRP
-    bar = pltpu.get_barrier_semaphore()
-    for k in range(1, PLN):
-        pl.semaphore_signal(bar, inc=1, device_id={"ep": ((grp + k) % PLN) * GRP + pos}, device_id_type=MESH)
-    pl.semaphore_wait(bar, PLN - 1)
-    for k in FAR:
-        peer = plane_peer(grp, k)
-        remote(y.at[peer], home.at[grp], row_s, row_r, peer * GRP + pos).start()
-    home[grp] = y[grp]
-
-    def pieces(g):
-        g1 = g.astype(jnp.bfloat16)
-        r1 = g - g1.astype(jnp.float32)
-        g2 = r1.astype(jnp.bfloat16)
-        g3 = (r1 - g2.astype(jnp.float32)).astype(jnp.bfloat16)
-        return jnp.concatenate([g1, g2, g3], axis=0)
-
-    def add(g, vals):
-        parts = jnp.dot(g, vals, preferred_element_type=F32)
-        return parts[:64] + (parts[64:128] + parts[128:])
-
-    w_c, w_h = pieces(gc[0:64, :]), pieces(gh[0:64, :])
-    for c in range(4):
-        cols = block_at(c, 512)
-        vals = cold[:, :, cols].reshape(512, 512)
-        acc[:, cols] = tok[:, cols].astype(jnp.float32) + add(w_c, vals)
-    drain(others(home), row_r)
-    for c in range(4):
-        cols = block_at(c, 512)
-        vals = home[:, :, cols].reshape(512, 512)
-        out[:, cols] = (acc[:, cols] + add(w_h, vals)).astype(jnp.bfloat16)
-    drain(others(home), row_s)
-
-
-def final_call(y, tokens, gh, gc, cold):
-    bf = jnp.bfloat16
-    vm = pl.BlockSpec(memory_space=VMEM)
-    return pl.pallas_call(
-        final_kernel,
-        out_shape=jax.ShapeDtypeStruct((64, MODEL), bf),
-        in_specs=[vm] * 5,
-        out_specs=vm,
-        scratch_shapes=[VMEM((PLN, 32, MODEL), bf), VMEM((64, MODEL), jnp.float32), pltpu.SemaphoreType.DMA, pltpu.SemaphoreType.DMA],
-        compiler_params=pltpu.CompilerParams(collective_id=1, **EFFECTS, vmem_limit_bytes=40 * MIB),
-    )(y, tokens, gh, gc, cold)
+        compiler_params=pltpu.CompilerParams(collective_id=0, **EFFECTS, vmem_limit_bytes=67043328),
+    )(tokens, ids_t, gat_t, counts, w_gate, w_up, w_down)
 
 
 def sparse_step(tokens, expert_ids, gate_w, route_counts, w_gate, w_up, w_down):
-    ids_t = jnp.concatenate([expert_ids.T, expert_ids.T], axis=1)
-    gat_t = jnp.concatenate([gate_w.T, gate_w.T], axis=1)
-    cnt_t = jnp.broadcast_to(route_counts, TILE)
-    rows_h, st, xr, cold, gh, gc, ok_all, info = main_call(tokens, ids_t, gat_t, cnt_t, w_gate, w_up, w_down)
-    y_h = hot_call(info, st, xr, w_gate, w_up, w_down, rows_h)
-    out = final_call(y_h.reshape(PLN, 32, MODEL), tokens, gh, gc, cold)
+    out, ok_all = main_call(tokens, expert_ids.T, gate_w.T, route_counts, w_gate, w_up, w_down)
     return out, jnp.min(ok_all) > 0.5
 
 

time: 187 us -> 165 us (0.88)
  Pallas kernels: 174 us -> 161 us
  local copies, waits for them, and re-layouts: 7.93 us -> 1.67 us
  other arithmetic: 4.32 us -> 1.46 us
    pallas_call x3 -> x1, Pallas kernels: 174 us -> 161 us  [main_call(): pl.pallas_call(main_kernel, out_shape=(jax.ShapeDtypeStruct((64, MODEL),...]
    unnamed x23 -> x1, local copies, waits for them, and re-layouts: 6.69 us -> 1.67 us
    concatenate x2 -> x0, other arithmetic: 2.85 us -> none  [the longest x1 1.43 us: sparse_step(): gat_t = jnp.concatenate([gate_w.T, gate_w.T], axis=1)]
where the time goes in v4:
time: 165 us
  Pallas kernels  161 us (98%)
  local copies, waits for them, and re-layouts  1.67 us (1%)
    pallas_call x1, Pallas kernels, main_call(): pl.pallas_call(main_kernel, out_shape=(jax.ShapeDtypeStruct((64, MODEL),...  161 us

profile of v4, /device:TPU:1, one launch (start us, length us, event | category | flops | bytes accessed | tf_op | source)
XLA Modules:
  0.0 164.6 jit_solution(12723645249964135223)
XLA Ops:
  0.0 160.6 %shard_map.75 = (bf16[64,2048]{1,0:T(8,128)(2,1)}, f32[16,8,128]{2,1,0:T(8,128)}) custom-call(bf16[64,2048]{1,0:T(8,128)(2,1)} %tok.1, s32[8,64]{1,0:T(8,128)} %bitcast.108, f32[8,64]{1,0:T(8,128)} %bitcast.109, s32[1,128]{1,0:T(1,128)} %cnt.1, bf16[1,2048,768]{2,1,0:T(8,128)(2,1)} %wg.1, bf16[1,2048,768]{2,1,0:T(8,128)(2,1)} %wu.1, bf16[1,768,2048]{2,1,0:T(8,128)(2,1)} %wd.1), custom_call_target="tpu_custom_call" | custom-call | tf_op jit(solution)/shard_map/pallas_call | solution.py:543
  160.6 1.5 reduce_min.9
  162.7 0.2 conditional.1
  162.9 1.7 %copy.33 = bf16[64,2048]{1,0:T(8,128)(2,1)} copy(bf16[64,2048]{1,0:T(8,128)(2,1)} %get-tuple-element.367) | data formatting | bytes 524288
